TPU v7x, 32 devices: a whole 2x2x4 slice. The times are simulated.
32 devices in a mesh: dp: 4 (over x, core), expert: 8 (over z, y).
Axes of the slice: x: 2, y: 2, z: 4, core: 2. Of those that a mesh axis runs over, the one named last changes fastest.
Arguments:
- tokens: bfloat16 [32768, 768], P(('dp', 'expert')), may hold values from -6 to 6
- segment: int32 [32768], P(('dp', 'expert')), may hold values from 0 to 15, as said below
- valid: int32 [32768], P(('dp', 'expert')), may hold values from 0 to 1, as said below
- routes: int32 [32768, 2], P(('dp', 'expert')), may hold values from 0 to 31, all different within a row
- out_grad: bfloat16 [32768, 768], P(('dp', 'expert')), may hold values from -6 to 6
- norm1_gain: float32 [768], P(('dp', 'expert')), may hold values from 0.5 to 1.5
- qkv_weight: float32 [2304, 768], P(('dp', 'expert')), may hold values from -0.21875 to 0.21875
- out_weight: float32 [768, 768], P(('dp', 'expert')), may hold values from -0.875 to 0.875
- norm2_gain: float32 [768], P(('dp', 'expert')), may hold values from 0.5 to 1.5
- router: float32 [768, 32], P(('dp', 'expert')), may hold values from -0.15625 to 0.15625
- train_in: float32 [16, 768, 3072], P('expert', None, 'dp'), may hold values from -0.21875 to 0.21875
- train_out: float32 [16, 768, 3072], P('expert', None, 'dp'), may hold values from -0.15625 to 0.15625
- frozen_in: float32 [16, 768, 3072], P('expert', None, 'dp'), may hold values from -0.21875 to 0.21875
- frozen_out: float32 [16, 768, 3072], P('expert', None, 'dp'), may hold values from -0.15625 to 0.15625
Outputs:
- output: bfloat16 [32768, 768], P(('dp', 'expert'))
- tokens_grad: bfloat16 [32768, 768], P(('dp', 'expert'))
- norm1_gain_grad: float32 [768], P(('dp', 'expert'))
- qkv_weight_grad: float32 [2304, 768], P(('dp', 'expert'))
- out_weight_grad: float32 [768, 768], P(('dp', 'expert'))
- norm2_gain_grad: float32 [768], P(('dp', 'expert'))
- router_grad: float32 [768, 32], P(('dp', 'expert'))
- train_in_grad: float32 [16, 768, 3072], P('expert', None, 'dp')
- train_out_grad: float32 [16, 768, 3072], P('expert', None, 'dp')
Inputs may be any that keep to these rules, and one draw needn't show every extreme that they name: `segment`: within each pack of 1024 consecutive tokens the sequence numbers start at 0, never fall and rise by one at each new sequence; every sequence fills a whole multiple of 64 tokens; in every draw some pack holds a single sequence and another holds only sequences of 64 tokens. `valid`: in each sequence the tokens are 1 except its last 0 to 31 tokens, which are 0. `routes`: the two experts of a row differ.
All inputs are finite; a program needn't handle non-finite values.
Results may differ from a plain program's by a relative error of at most 0.014.
Values may be sent and summed in bfloat16 or wider, within the bound.
A program may use at most 320 MiB of HBM per device.

v0:
```python
import jax
import jax.numpy as jnp
from jax import lax
from jax.sharding import PartitionSpec as P

HD = 64
CAP = 96


epsilon = 1e-05
masked_score = -1e30


def layer_norm(values):
    centre = jnp.mean(values, axis=-1, keepdims=True)
    centred = values - centre
    spread = jnp.mean(centred * centred, axis=-1, keepdims=True)
    return centred * lax.rsqrt(spread + epsilon)


def gelu_tanh(values):
    return jax.nn.gelu(values, approximate=True)


def slot_table(route_ids, valid_ids, expert_count, capacity):
    pair_ids = route_ids.reshape(-1)
    pair_live = jnp.repeat(valid_ids, 2) > 0
    onehot = (
        (pair_ids[:, None] == jnp.arange(expert_count, dtype=jnp.int32)[None, :])
        & pair_live[:, None]
    ).astype(jnp.int32)
    earlier = jnp.cumsum(onehot, axis=0, dtype=jnp.int32) - onehot
    slot_ids = jnp.sum(earlier * onehot, axis=1, dtype=jnp.int32)
    kept = pair_live & (slot_ids < capacity)
    return (slot_ids.reshape(-1, 2), kept.reshape(-1, 2))


def seen_pairs(seg_ids, valid_ids, row_start, row_stop):
    rows_here = jnp.arange(row_start, row_stop, dtype=jnp.int32)[:, None]
    keys_here = jnp.arange(row_stop, dtype=jnp.int32)[None, :]
    same_segment = seg_ids[row_start:row_stop, None] == seg_ids[None, :row_stop]
    return same_segment & (keys_here <= rows_here) & (valid_ids[None, :row_stop] > 0)


def attend_forward(query, key_rows, value_rows, seg_ids, valid_ids, head_count):
    row_count = query.shape[0]
    block_rows = min(512, row_count)
    scale = HD ** (-0.5)
    out_blocks = []
    log_sums = []
    for row_start in range(0, row_count, block_rows):
        row_stop = row_start + block_rows
        query_head = query[row_start:row_stop].reshape(block_rows, head_count, HD)
        key_head = key_rows[:row_stop].reshape(row_stop, head_count, HD)
        value_head = value_rows[:row_stop].reshape(row_stop, head_count, HD)
        scores = (
            jnp.einsum("qhd,khd->hqk", query_head, key_head, preferred_element_type=jnp.float32)
            * scale
        )
        scores = jnp.where(
            seen_pairs(seg_ids, valid_ids, row_start, row_stop)[None], scores, masked_score
        )
        row_max = jnp.max(scores, axis=-1, keepdims=True)
        exponent = jnp.exp(scores - row_max)
        row_total = jnp.sum(exponent, axis=-1, keepdims=True)
        attention = (exponent / row_total).astype(jnp.bfloat16)
        combined = jnp.einsum(
            "hqk,khd->qhd", attention, value_head, preferred_element_type=jnp.float32
        )
        out_blocks.append(combined.reshape(block_rows, head_count * HD).astype(jnp.bfloat16))
        log_sums.append(row_max + jnp.log(row_total))
    return (jnp.concatenate(out_blocks, axis=0), log_sums)


def attend_backward(query, key_rows, value_rows, d_heads, seg_ids, valid_ids, log_sums, head_count):
    row_count = query.shape[0]
    block_rows = min(512, row_count)
    scale = HD ** (-0.5)
    d_query_blocks = []
    d_key = jnp.zeros((row_count, head_count, HD), jnp.float32)
    d_value = jnp.zeros((row_count, head_count, HD), jnp.float32)
    for block_number, row_start in enumerate(range(0, row_count, block_rows)):
        row_stop = row_start + block_rows
        query_head = query[row_start:row_stop].reshape(block_rows, head_count, HD)
        key_head = key_rows[:row_stop].reshape(row_stop, head_count, HD)
        value_head = value_rows[:row_stop].reshape(row_stop, head_count, HD)
        grad_head = d_heads[row_start:row_stop].reshape(block_rows, head_count, HD)
        scores = (
            jnp.einsum("qhd,khd->hqk", query_head, key_head, preferred_element_type=jnp.float32)
            * scale
        )
        scores = jnp.where(
            seen_pairs(seg_ids, valid_ids, row_start, row_stop)[None], scores, masked_score
        )
        attention = jnp.exp(scores - log_sums[block_number])
        d_attention = jnp.einsum(
            "qhd,khd->hqk", grad_head, value_head, preferred_element_type=jnp.float32
        )
        d_scores = (
            attention * (d_attention - jnp.sum(d_attention * attention, axis=-1, keepdims=True))
        ).astype(jnp.bfloat16)
        d_query_blocks.append(
            (
                jnp.einsum("hqk,khd->qhd", d_scores, key_head, preferred_element_type=jnp.float32)
                * scale
            ).reshape(block_rows, head_count * HD)
        )
        d_key = d_key.at[:row_stop].add(
            jnp.einsum("hqk,qhd->khd", d_scores, query_head, preferred_element_type=jnp.float32)
            * scale
        )
        d_value = d_value.at[:row_stop].add(
            jnp.einsum(
                "hqk,qhd->khd",
                attention.astype(jnp.bfloat16),
                grad_head,
                preferred_element_type=jnp.float32,
            )
        )
    d_query = jnp.concatenate(d_query_blocks, axis=0).astype(jnp.bfloat16)
    return (
        d_query,
        d_key.reshape(row_count, head_count * HD).astype(jnp.bfloat16),
        d_value.reshape(row_count, head_count * HD).astype(jnp.bfloat16),
    )


def expert_forward(row_data, weight_in, weight_out):
    inner = jnp.einsum("nlcd,ldf->nlcf", row_data, weight_in, preferred_element_type=jnp.float32)
    active = gelu_tanh(inner).astype(jnp.bfloat16)
    return jnp.einsum(
        "nlcf,ldf->nlcd", active, weight_out, preferred_element_type=jnp.float32
    ).astype(jnp.bfloat16)


def expert_inner_grad(row_data, d_rows, weight_in, weight_out):
    inner = jnp.einsum("nlcd,ldf->nlcf", row_data, weight_in, preferred_element_type=jnp.float32)
    active, gelu_pull = jax.vjp(gelu_tanh, inner)
    d_active = jnp.einsum("nlcd,ldf->nlcf", d_rows, weight_out, preferred_element_type=jnp.float32)
    d_inner = gelu_pull(d_active)[0].astype(jnp.bfloat16)
    d_input = jnp.einsum(
        "nlcf,ldf->nlcd", d_inner, weight_in, preferred_element_type=jnp.float32
    ).astype(jnp.bfloat16)
    return (active.astype(jnp.bfloat16), d_inner, d_input)


def local(
    tokens,
    segment,
    valid,
    routes,
    out_grad,
    norm1_gain,
    qkv_weight,
    out_weight,
    norm2_gain,
    router,
    train_in,
    train_out,
    frozen_in,
    frozen_out,
):
    model_width = tokens.shape[1]
    head_count = model_width // HD
    expert_count = router.shape[1]
    groups = lax.axis_size("expert")
    local_count = expert_count // groups
    dense_low = (
        lax.all_gather(norm1_gain.astype(jnp.bfloat16), ("dp", "expert"), axis=0, tiled=True),
        lax.all_gather(qkv_weight.astype(jnp.bfloat16), ("dp", "expert"), axis=0, tiled=True),
        lax.all_gather(out_weight.astype(jnp.bfloat16), ("dp", "expert"), axis=0, tiled=True),
        lax.all_gather(norm2_gain.astype(jnp.bfloat16), ("dp", "expert"), axis=0, tiled=True),
        lax.all_gather(router.astype(jnp.bfloat16), ("dp", "expert"), axis=0, tiled=True),
    )
    gain_one, projections, attention_out, gain_two, router_low = dense_low
    gain_one = gain_one.astype(jnp.float32)
    gain_two = gain_two.astype(jnp.float32)
    projection_stack = projections.reshape(3, model_width, model_width)
    experts_low = (
        lax.all_gather(train_in.astype(jnp.bfloat16), "dp", axis=2, tiled=True),
        lax.all_gather(train_out.astype(jnp.bfloat16), "dp", axis=2, tiled=True),
        lax.all_gather(frozen_in.astype(jnp.bfloat16), "dp", axis=2, tiled=True),
        lax.all_gather(frozen_out.astype(jnp.bfloat16), "dp", axis=2, tiled=True),
    )
    tokens_f = tokens.astype(jnp.float32)
    valid_f = valid.astype(jnp.float32)[:, None]
    norm_one = layer_norm(tokens_f)
    act = (norm_one * gain_one).astype(jnp.bfloat16)
    projected = jnp.einsum(
        "td,jde->jte", act, projection_stack, preferred_element_type=jnp.float32
    ).astype(jnp.bfloat16)
    query, key_rows, value_rows = (projected[0], projected[1], projected[2])
    heads_out, log_sums = attend_forward(query, key_rows, value_rows, segment, valid, head_count)
    attn = jnp.dot(heads_out, attention_out, preferred_element_type=jnp.float32) * valid_f
    resid = tokens_f + attn
    norm_two = layer_norm(resid)
    hidden = (norm_two * gain_two).astype(jnp.bfloat16)
    logits = jnp.dot(hidden, router_low, preferred_element_type=jnp.float32)
    soft = jax.nn.softmax(logits, axis=-1)
    choose = (
        routes[:, :, None] == jnp.arange(expert_count, dtype=jnp.int32)[None, None, :]
    ).astype(jnp.float32)
    picked = jnp.sum(soft[:, None, :] * choose, axis=2)
    picked_total = jnp.sum(picked, axis=1, keepdims=True)
    gates = picked / picked_total
    slot_ids, kept = slot_table(routes, valid, expert_count, CAP)
    kept_f = kept.astype(jnp.float32)
    dest = jnp.where(kept, routes * CAP + slot_ids, expert_count * CAP)
    flat_dest = dest.reshape(-1)
    send_rows = (
        jnp.zeros((expert_count * CAP + 1, model_width), jnp.bfloat16)
        .at[flat_dest]
        .add(jnp.repeat(hidden, 2, axis=0))
    )
    send_rows = send_rows[:-1].reshape(groups, local_count, CAP, model_width)
    arrived = lax.all_to_all(send_rows, "expert", split_axis=0, concat_axis=0, tiled=True)
    arrived_split = arrived.reshape(groups, local_count // 2, 2, CAP, model_width)
    rows_train = arrived_split[:, :, 0]
    rows_frozen = arrived_split[:, :, 1]
    out_train = expert_forward(rows_train, experts_low[0], experts_low[1])
    out_frozen = expert_forward(rows_frozen, experts_low[2], experts_low[3])
    expert_out = jnp.stack([out_train, out_frozen], axis=2).reshape(
        groups, local_count, CAP, model_width
    )
    returned = lax.all_to_all(
        expert_out, "expert", split_axis=0, concat_axis=0, tiled=True
    ).reshape(expert_count * CAP, model_width)
    chosen = jnp.take(returned, dest, axis=0, mode="fill", fill_value=0)
    mixture = jnp.einsum("tkd,tk->td", chosen, gates * kept_f, preferred_element_type=jnp.float32)
    output = ((resid + mixture) * valid_f).astype(jnp.bfloat16)
    cotangent = out_grad.astype(jnp.float32) * valid_f
    d_gate = kept_f * jnp.einsum(
        "td,tkd->tk", cotangent, chosen, preferred_element_type=jnp.float32
    )
    d_chosen = ((gates * kept_f)[:, :, None] * cotangent[:, None, :]).astype(jnp.bfloat16)
    d_send = (
        jnp.zeros((expert_count * CAP + 1, model_width), jnp.bfloat16)
        .at[flat_dest]
        .add(d_chosen.reshape(-1, model_width))
    )
    d_send = d_send[:-1].reshape(groups, local_count, CAP, model_width)
    d_arrived = lax.all_to_all(d_send, "expert", split_axis=0, concat_axis=0, tiled=True)
    d_split = d_arrived.reshape(groups, local_count // 2, 2, CAP, model_width)
    experts_back = (
        lax.all_gather(train_in.astype(jnp.bfloat16), "dp", axis=2, tiled=True),
        lax.all_gather(train_out.astype(jnp.bfloat16), "dp", axis=2, tiled=True),
        lax.all_gather(frozen_in.astype(jnp.bfloat16), "dp", axis=2, tiled=True),
        lax.all_gather(frozen_out.astype(jnp.bfloat16), "dp", axis=2, tiled=True),
    )
    active_train, d_inner_train, d_input_train = expert_inner_grad(
        rows_train, d_split[:, :, 0], experts_back[0], experts_back[1]
    )
    grad_train_out = jnp.einsum(
        "nlcd,nlcf->ldf", d_split[:, :, 0], active_train, preferred_element_type=jnp.float32
    )
    grad_train_in = jnp.einsum(
        "nlcd,nlcf->ldf", rows_train, d_inner_train, preferred_element_type=jnp.float32
    )
    active_frozen, d_inner_frozen, d_input_frozen = expert_inner_grad(
        rows_frozen, d_split[:, :, 1], experts_back[2], experts_back[3]
    )
    d_expert_in = jnp.stack([d_input_train, d_input_frozen], axis=2).reshape(
        groups, local_count, CAP, model_width
    )
    d_returned = lax.all_to_all(
        d_expert_in, "expert", split_axis=0, concat_axis=0, tiled=True
    ).reshape(expert_count * CAP, model_width)
    d_taken = jnp.take(d_returned, dest, axis=0, mode="fill", fill_value=0)
    d_hidden = jnp.sum(d_taken.astype(jnp.float32), axis=1)
    d_picked = (d_gate - jnp.sum(d_gate * gates, axis=1, keepdims=True)) / picked_total
    d_soft = jnp.sum(d_picked[:, :, None] * choose, axis=1)
    d_logits = (soft * (d_soft - jnp.sum(d_soft * soft, axis=-1, keepdims=True))).astype(
        jnp.bfloat16
    )
    grad_router = jnp.dot(hidden.T, d_logits, preferred_element_type=jnp.float32)
    d_hidden = d_hidden + jnp.dot(d_logits, router_low.T, preferred_element_type=jnp.float32)
    grad_gain_two = jnp.sum(d_hidden * norm_two, axis=0)
    norm_two_pull = jax.vjp(layer_norm, resid)[1]
    d_resid = cotangent + norm_two_pull(d_hidden * gain_two)[0]
    d_attn = (d_resid * valid_f).astype(jnp.bfloat16)
    grad_attention_out = jnp.dot(heads_out.T, d_attn, preferred_element_type=jnp.float32)
    d_heads = jnp.dot(d_attn, attention_out.T, preferred_element_type=jnp.float32).astype(
        jnp.bfloat16
    )
    d_query, d_key, d_value = attend_backward(
        query, key_rows, value_rows, d_heads, segment, valid, log_sums, head_count
    )
    d_projected = jnp.stack([d_query, d_key, d_value], axis=0)
    grad_projections = jnp.einsum(
        "td,jte->jde", act, d_projected, preferred_element_type=jnp.float32
    ).reshape(3 * model_width, model_width)
    d_act = jnp.einsum(
        "jte,jde->td", d_projected, projection_stack, preferred_element_type=jnp.float32
    )
    grad_gain_one = jnp.sum(d_act * norm_one, axis=0)
    norm_one_pull = jax.vjp(layer_norm, tokens_f)[1]
    tokens_grad = (d_resid + norm_one_pull(d_act * gain_one)[0]).astype(jnp.bfloat16)
    dense_sums = (
        lax.psum_scatter(grad_gain_one, ("dp", "expert"), scatter_dimension=0, tiled=True),
        lax.psum_scatter(grad_projections, ("dp", "expert"), scatter_dimension=0, tiled=True),
        lax.psum_scatter(grad_attention_out, ("dp", "expert"), scatter_dimension=0, tiled=True),
        lax.psum_scatter(grad_gain_two, ("dp", "expert"), scatter_dimension=0, tiled=True),
        lax.psum_scatter(grad_router, ("dp", "expert"), scatter_dimension=0, tiled=True),
    )
    expert_sums = (
        lax.psum_scatter(
            grad_train_in.astype(jnp.bfloat16), "dp", scatter_dimension=2, tiled=True
        ).astype(jnp.float32),
        lax.psum_scatter(
            grad_train_out.astype(jnp.bfloat16), "dp", scatter_dimension=2, tiled=True
        ).astype(jnp.float32),
    )
    return (
        output,
        tokens_grad,
        dense_sums[0],
        dense_sums[1],
        dense_sums[2],
        dense_sums[3],
        dense_sums[4],
        expert_sums[0],
        expert_sums[1],
    )


def solution(mesh):
    placed = (
        P(("dp", "expert"), None),
        P(("dp", "expert")),
        P(("dp", "expert")),
        P(("dp", "expert"), None),
        P(("dp", "expert"), None),
        P(("dp", "expert")),
        P(("dp", "expert"), None),
        P(("dp", "expert"), None),
        P(("dp", "expert")),
        P(("dp", "expert"), None),
        P("expert", None, "dp"),
        P("expert", None, "dp"),
        P("expert", None, "dp"),
        P("expert", None, "dp"),
    )
    return jax.shard_map(
        local,
        mesh=mesh,
        in_specs=placed,
        out_specs=(
            P(("dp", "expert"), None),
            P(("dp", "expert"), None),
            P(("dp", "expert")),
            P(("dp", "expert"), None),
            P(("dp", "expert"), None),
            P(("dp", "expert")),
            P(("dp", "expert"), None),
            P("expert", None, "dp"),
            P("expert", None, "dp"),
        ),
        check_vma=False,
    )
```

profile of v0, /device:TPU:0, one launch (start us, length us, event | category | flops | bytes accessed | tf_op | source)
XLA Modules:
  0.0 1329.0 jit_solution(10538978052750243825)
XLA Ops:
  10.5 3.9 convert_element_type.235
  14.5 4.0 convert_element_type.230
  18.6 4.0 convert_element_type.237
  24.0 42.7 %all-reduce.8 = (bf16[768]{0:T(1024)(128)(2,1)S(1)}, bf16[768]{0:T(1024)(128)(2,1)S(1)}) all-reduce(bf16[768]{0:T(1024)(128)(2,1)S(1)} %dynamic-update-slice.10, bf16[768]{0:T(1024)(128)(2,1)S(1)} %dynamic-update-slice.11), channel_id=1, replica_groups=mesh['dp'=4,'expert'=8] {'dp','expert'}, use_global_device_ids=true, to_apply=%add.2 | all-reduce | flops 1536 | bytes 6144
  67.7 9.1 reduce-window.6
  83.3 6.5 convert_bitcast_fusion
  99.6 12.1 fusion.51
  111.7 13.5 %fusion = f32[12,512]{1,0:T(8,128)S(1)} fusion(f32[12,512]{1,0:T(8,128)S(1)} %get-tuple-element.154, f32[12,512,1024]{2,1,0:T(8,128)} %get-tuple-element.155, pred[512,1024]{1,0:T(8,128)(4,1)S(1)} %copy-done.20), kind=kLoop, calls=%fused_computation.14 | loop fusion | flops 25159680 | bytes 25739264 | tf_op jit(solution)/shard_map/reduce_sum | solution.py:65
  125.4 7.7 fusion.94
  135.6 8.8 fusion.95
  144.4 3.6 fusion.145
  154.7 7.6 reshape.625
  162.2 18.2 %scatter_custom_fusion = bf16[3073,768]{1,0:T(8,128)(2,1)} fusion(s32[2048]{0:T(1024)S(1)} %bitcast.295, bf16[2048,768]{1,0:T(8,128)(2,1)} %reshape.625, bf16[]{:T(256)} %constant.173.clone.1), kind=kCustom, calls=%fused_computation.123 | custom fusion | flops 1572864 | bytes 4720640 | tf_op jit(solution)/shard_map/scatter-add | solution.py:213
  180.4 4.8 slice.187
  185.2 5.3 all-to-all-start
  190.6 4.0 convert_element_type.232
  194.6 99.8 %all-to-all-done = bf16[8,4,96,768]{3,2,1,0:T(8,128)(2,1)} async-done(((bf16[8,4,96,768]{3,2,1,0:T(8,128)(2,1)}), bf16[8,4,96,768]{3,2,1,0:T(8,128)(2,1)}, u32[]{:S(2)}, u32[]{:S(2)}) %all-to-all-start) | async-done | bytes 4718624 | tf_op jit(solution)/shard_map/all_to_all | solution.py:216
  294.5 4.3 fusion.140
  298.8 16.4 %fusion.32 = f32[2,8,96,3072]{3,2,1,0:T(8,128)} fusion(bf16[2,768,3072]{2,1,0:T(8,128)(2,1)} %all-gather.15.cloned.1.call-done, bf16[8,2,1,96,768]{4,3,2,1,0:T(8,128)(2,1)} %get-tuple-element.140), kind=kOutput, calls=%fused_computation.59 | convolution fusion | flops 7247757312 | bytes 30670848 | tf_op jit(solution)/shard_map/nlcd,ldf->nlcf/dot_general | solution.py:129
  315.2 14.2 %fusion.40 = f32[2,8,96,3072]{3,2,1,0:T(8,128)} fusion(bf16[2,768,3072]{2,1,0:T(8,128)(2,1)} %all-gather.11.cloned.1.call-done, bf16[8,2,1,96,768]{4,3,2,1,0:T(8,128)(2,1)S(1)} %get-tuple-element.139), kind=kOutput, calls=%fused_computation.67 | convolution fusion | flops 7247757312 | bytes 30670848 | tf_op jit(solution)/shard_map/nlcd,ldf->nlcf/dot_general | solution.py:129
  329.4 16.2 %convert_bitcast_fusion.3 = bf16[8,2,1,96,768]{4,3,0,1,2:T(8,128)(2,1)S(1)} fusion(bf16[2,768,3072]{2,1,0:T(8,128)(2,1)} %all-gather.17.cloned.1.call-done, f32[2,8,96,3072]{3,2,1,0:T(8,128)} %fusion.32), kind=kOutput, calls=%fused_computation.131 | convolution fusion | flops 7291404288 | bytes 30670848 | tf_op jit(solution)/shard_map/nlcf,ldf->nlcd/dot_general | solution.py:131
  345.6 47.5 %all-gather.13.cloned.1.call-done = bf16[2,768,3072]{2,1,0:T(8,128)(2,1)} async-done(((bf16[2,768,768]{2,1,0:T(8,128)(2,1)}), bf16[2,768,3072]{2,1,0:T(8,128)(2,1)}) %all-gather.13.cloned.1.call-update) | async-done | bytes 9437200 | tf_op jit(solution)/shard_map/all_gather | solution.py:181
  393.1 16.9 %convert_bitcast_fusion.4 = bf16[8,2,1,96,768]{4,3,0,1,2:T(8,128)(2,1)} fusion(bf16[2,768,3072]{2,1,0:T(8,128)(2,1)} %all-gather.13.cloned.1.call-done, f32[2,8,96,3072]{3,2,1,0:T(8,128)} %fusion.40), kind=kOutput, calls=%fused_computation.132 | convolution fusion | flops 7291404288 | bytes 30670848 | tf_op jit(solution)/shard_map/nlcf,ldf->nlcd/dot_general | solution.py:131
  414.7 5.7 all-to-all-start.1
  427.7 5.0 mul.356
  432.7 8.5 mul.357
  441.2 140.3 %all_gather.39 = bf16[768,32]{1,0:T(8,128)(2,1)S(1)} all-gather(bf16[24,32]{1,0:T(8,128)(2,1)S(1)} %convert_element_type.240), channel_id=1, replica_groups=mesh['dp'=4,'expert'=8] {'dp','expert'}, dimensions={0}, use_global_device_ids=true | all-gather | bytes 50688 | tf_op jit(solution)/shard_map/all_gather | solution.py:173
  584.7 13.4 %gather_fusion = bf16[2048,768]{1,0:T(8,128)(2,1)} fusion(bf16[3072,768]{1,0:T(8,128)(2,1)} %bitcast.37, s32[2048]{0:T(1024)S(1)} %broadcast_clamp_fusion), kind=kCustom, calls=%fused_computation.clone | custom fusion | bytes 6299648 | tf_op jit(solution)/shard_map/jit(_take)/gather | solution.py:228
  598.2 6.1 reshape.648
  604.3 16.8 %multiply_reduce_fusion.2 = f32[1024,2]{1,0:T(8,128)} fusion(f32[1024,768]{1,0:T(8,128)} %copy-done.12, bf16[1024,2,768]{2,1,0:T(2,128)(2,1)S(1)} %reshape.648, pred[1024,2]{1,0:T(8,128)(4,1)S(1)} %copy.153), kind=kLoop, calls=%fused_computation.78 | loop fusion | flops 6289408 | bytes 6301696
  625.4 18.9 %scatter_custom_fusion.1 = bf16[3073,768]{1,0:T(8,128)(2,1)} fusion(s32[2048]{0:T(1024)S(1)} %bitcast.296, f32[2048,768]{1,0:T(8,128)} %mul.357, f32[2048]{0:T(1024)S(1)} %and_select_fusion, bf16[]{:T(256)} %constant.173.clone.1), kind=kCustom, calls=%fused_computation.106 | custom fusion | flops 4718592 | bytes 11019778 | tf_op jit(solution)/shard_map/scatter-add | solution.py:239
  646.6 104.6 %all_to_all.20 = bf16[8,4,96,768]{3,2,1,0:T(8,128)(2,1)S(1)} all-to-all(bf16[8,4,96,768]{3,2,1,0:T(8,128)(2,1)S(1)} %bitcast.266), channel_id=1, replica_groups=mesh['dp'=4,'expert'=8] {'expert'}, dimensions={0} | all-to-all | bytes 9437184 | tf_op jit(solution)/shard_map/all_to_all | solution.py:242
  754.3 14.7 %bitcast_convert_fusion = bf16[2,768,3072]{2,1,0:T(8,128)(2,1)} fusion(bf16[8,2,1,96,768]{4,3,2,1,0:T(8,128)(2,1)S(1)} %get-tuple-element.137, f32[2,8,96,3072]{3,2,1,0:T(8,128)} %fusion.40), kind=kOutput, calls=%fused_computation.30 | convolution fusion | flops 7294943232 | bytes 30670848 | tf_op jit(solution)/shard_map/nlcd,nlcf->ldf/dot_general | solution.py:253
  769.0 22.4 %fusion.8 = bf16[8,2,96,3072]{3,2,0,1:T(8,128)(2,1)S(1)} fusion(f32[2,8,96,3072]{3,2,1,0:T(8,128)} %fusion.40, bf16[2,768,3072]{2,1,0:T(8,128)(2,1)} %all-gather.13.cloned.1.call-done, bf16[8,2,1,96,768]{4,3,2,1,0:T(8,128)(2,1)} %copy-done.38), kind=kOutput, calls=%fused_computation.22 | convolution fusion | flops 7342129152 | bytes 40108032 | tf_op jit(solution)/shard_map/nlcd,ldf->nlcf/dot_general | solution.py:139
  791.5 3.6 copy-done.109
  795.1 10.2 bitcast_convert_fusion.1
  806.9 14.6 %fusion.34 = f32[2,8,96,3072]{3,2,1,0:T(8,128)} fusion(bf16[2,768,3072]{2,1,0:T(8,128)(2,1)} %all-gather.17.cloned.1.call-done, bf16[8,2,1,96,768]{4,3,2,1,0:T(8,128)(2,1)S(1)} %copy-done.37), kind=kOutput, calls=%fused_computation.61 | convolution fusion | flops 7247757312 | bytes 30670848 | tf_op jit(solution)/shard_map/nlcd,ldf->nlcf/dot_general | solution.py:139
  821.6 10.3 convert_bitcast_fusion.2
  831.8 25.0 %convert_bitcast_fusion.1 = bf16[8,2,1,96,768]{4,3,0,1,2:T(8,128)(2,1)} fusion(bf16[2,768,3072]{2,1,0:T(8,128)(2,1)} %all-gather.15.cloned.1.call-done, f32[2,8,96,3072]{3,2,1,0:T(8,128)} %fusion.34, f32[2,8,96,3072]{3,2,1,0:T(8,128)} %fusion.32), kind=kOutput, calls=%fused_computation.129 | convolution fusion | flops 7343308800 | bytes 49545216 | tf_op jit(solution)/shard_map/nlcf,ldf->nlcd/dot_general | solution.py:141
  863.0 4.9 all-to-all-start.3
  870.7 100.7 %all-to-all-done.3 = bf16[8,4,96,768]{3,2,1,0:T(8,128)(2,1)} async-done(((bf16[8,4,96,768]{3,2,1,0:T(8,128)(2,1)}), bf16[8,4,96,768]{3,2,1,0:T(8,128)(2,1)}, u32[]{:S(2)}, u32[]{:S(2)}) %all-to-all-start.3) | async-done | bytes 4718624 | tf_op jit(solution)/shard_map/all_to_all | solution.py:265
  971.4 13.4 %gather_fusion.1 = bf16[2048,768]{1,0:T(8,128)(2,1)} fusion(bf16[3072,768]{1,0:T(8,128)(2,1)} %bitcast.53, s32[2048]{0:T(1024)S(1)} %copy-done.3), kind=kCustom, calls=%fused_computation.1.clone | custom fusion | bytes 6299648 | tf_op jit(solution)/shard_map/jit(_take)/gather | solution.py:268
  984.8 7.4 reshape.652
  992.2 23.0 %convert_reduce_fusion = (f32[1024,768]{1,0:T(8,128)}, f32[1024,768]{1,0:T(8,128)}) fusion(bf16[1024,2,768]{2,1,0:T(2,128)(2,1)} %reshape.652, pred[1024,2]{1,0:T(8,128)(4,1)S(1)} %copy-done.47, f32[1024,2]{1,0:T(8,128)} %copy.206, bf16[1024,2,768]{2,1,0:T(2,128)(2,1)S(1)} %copy-done.11), kind=kLoop, calls=%fused_computation.81 | loop fusion | flops 9437184 | bytes 12593152 | tf_op jit(solution)/shard_map/reduce_sum | solution.py:269
  1015.2 3.7 copy.168
  1019.0 4.6 multiply_reduce_fusion.4
  1023.6 3.6 copy.188
  1027.1 5.2 fusion.138
  1037.1 4.0 fusion.91
  1041.1 6.9 multiply_reduce_fusion.1
  1048.0 20.2 %multiply_reduce_fusion = (f32[12,512]{1,0:T(8,128)S(1)}, f32[12,512,1024]{2,1,0:T(8,128)}) fusion(f32[12,512]{1,0:T(8,128)S(1)} %log_add_fusion, f32[12,512,1024]{2,1,0:T(8,128)} %get-tuple-element.155, pred[512,1024]{1,0:T(8,128)(4,1)S(1)} %copy-done.21, bf16[512,12,64]{0,2,1:T(8,128)(2,1)S(1)} %bitcast.289, bf16[1024,12,64]{0,2,1:T(8,128)(2,1)} %bitcast.282), kind=kOutput, calls=%fused_computation.9 | convolution fusion | flops 836757504 | bytes 53264384 | tf_op jit(solution)/shard_map/qhd,khd->hqk/dot_general | solution.py:96
  1068.1 13.4 %fusion.68 = bf16[1024,12,64]{0,2,1:T(8,128)(2,1)} fusion(f32[512,12,64]{0,2,1:T(8,128)} %fusion.91, bf16[512,12,64]{0,2,1:T(8,128)(2,1)S(1)} %bitcast.290, f32[12,512]{1,0:T(8,128)S(1)} %log_add_fusion, f32[12,512,1024]{2,1,0:T(8,128)} %get-tuple-element.155, pred[512,1024]{1,0:T(8,128)(4,1)S(1)} %copy-done.21), kind=kOutput, calls=%fused_computation.109 | convolution fusion | flops 832045056 | bytes 29646848 | tf_op jit(solution)/shard_map/hqk,qhd->khd/dot_general | solution.py:113
  1081.5 7.0 multiply_convert_fusion.1
  1098.3 17.9 %multiply_convert_fusion = bf16[12,512,1024]{2,1,0:T(8,128)(2,1)S(1)} fusion(f32[12,512,1024]{2,1,0:T(8,128)} %get-tuple-element.166, f32[12,512]{1,0:T(8,128)S(1)} %get-tuple-element.165, f32[12,512]{1,0:T(8,128)S(1)} %log_add_fusion, f32[12,512,1024]{2,1,0:T(8,128)} %get-tuple-element.155, pred[512,1024]{1,0:T(8,128)(4,1)} %fusion.75), kind=kLoop, calls=%fused_computation.8 | loop fusion | flops 37748736 | bytes 63488000 | tf_op jit(solution)/shard_map/convert_element_type | solution.py:101
  1116.3 7.4 multiply_convert_fusion.7
  1126.1 5.2 multiply_bitcast_fusion
  1131.3 7.2 fusion.69
  1140.1 9.1 fusion.99
  1152.4 7.4 fusion.66
  1162.8 38.4 %all-reduce.7 = (f32[768]{0:T(1024)S(1)}, f32[768]{0:T(1024)S(1)}) all-reduce(f32[768]{0:T(1024)S(1)} %get-tuple-element.121, f32[768]{0:T(1024)S(1)} %get-tuple-element.119), channel_id=2, replica_groups=mesh['dp'=4,'expert'=8] {'dp','expert'}, use_global_device_ids=true, to_apply=%region_28.30.clone | all-reduce | flops 1536 | bytes 12288
  1202.4 5.6 add_convert_fusion
  1210.6 4.3 convert_element_type.266
  1214.9 4.3 convert_element_type.264
  1219.2 102.9 %reduce-scatter.8.cloned.1.call-done = f32[72,768]{1,0:T(8,128)} async-done(((f32[2304,768]{1,0:T(8,128)}), f32[72,768]{1,0:T(8,128)}) %reduce-scatter.8.cloned.1.call-update) | async-done | bytes 221200 | tf_op jit(solution)/shard_map/reduce_scatter | solution.py:300
  (377 shorter events, 94.3 us)
Async XLA Ops:
  7.2 76.1 %all-gather.7.cloned.1.call-start = ((), (), s32[]{:S(2)}) async-start(), calls=%async_computation.9 | async-start | bytes 3649536 | tf_op jit(solution)/shard_map/all_gather | solution.py:170
  8.8 135.6 %all-gather.9.cloned.1.call-start = ((), (), s32[]{:S(2)}) async-start(), calls=%async_computation.10 | async-start | bytes 1216512 | tf_op jit(solution)/shard_map/all_gather | solution.py:171
  10.4 288.3 %all-gather.15.cloned.1.call-start = ((), (), s32[]{:S(2)}) async-start(), calls=%async_computation.13 | async-start | bytes 11796480 | tf_op jit(solution)/shard_map/all_gather | solution.py:182
  14.4 300.8 %all-gather.11.cloned.1.call-start = ((), (), s32[]{:S(2)}) async-start(), calls=%async_computation.11 | async-start | bytes 11796480 | tf_op jit(solution)/shard_map/all_gather | solution.py:180
  18.6 48.3 %copy-start.100 = (s32[1024]{0:T(1024)S(1)}, s32[1024]{0:T(1024)}, u32[]{:S(2)}) copy-start(s32[1024]{0:T(1024)} %param.29) | copy-start | bytes 12292
  18.6 310.8 %all-gather.17.cloned.1.call-start = ((), (), s32[]{:S(2)}) async-start(), calls=%async_computation.14 | async-start | bytes 11796480 | tf_op jit(solution)/shard_map/all_gather | solution.py:183
  22.6 56.8 %copy-start.41 = (bf16[1024,768]{1,0:T(8,128)(2,1)S(1)}, bf16[1024,768]{1,0:T(8,128)(2,1)}, u32[]{:S(2)}) copy-start(bf16[1024,768]{1,0:T(8,128)(2,1)} %param.28) | copy-start | bytes 4718596
  22.7 59.1 %copy-start.84 = (pred[1024]{0:T(1024)(128)(4,1)}, pred[1024]{0:T(1024)(128)(4,1)S(1)}, u32[]{:S(2)}) copy-start(pred[1024]{0:T(1024)(128)(4,1)S(1)} %broadcast_compare_fusion) | copy-start | bytes 3076
  22.7 399.2 %copy-start.64 = (f32[1024]{0:T(1024)}, f32[1024]{0:T(1024)S(1)}, u32[]{:S(2)}) copy-start(f32[1024]{0:T(1024)S(1)} %convert_element_type.224) | copy-start | bytes 12292
  66.8 16.5 %copy-start.87 = (f32[768]{0:T(1024)}, f32[768]{0:T(1024)S(1)}, u32[]{:S(2)}) copy-start(f32[768]{0:T(1024)S(1)} %convert_element_type.210) | copy-start | bytes 9220
  66.8 81.7 %copy-start.80 = (f32[768]{0:T(1024)}, f32[768]{0:T(1024)S(1)}, u32[]{:S(2)}) copy-start(f32[768]{0:T(1024)S(1)} %convert_element_type.228) | copy-start | bytes 9220
  67.6 13.4 %copy-start.98 = (pred[2048]{0:T(1024)(128)(4,1)}, pred[2048]{0:T(1024)(128)(4,1)S(1)}, u32[]{:S(2)}) copy-start(pred[2048]{0:T(1024)(128)(4,1)S(1)} %gt.33) | copy-start | bytes 6148
  80.3 64.2 %copy-start.8 = (bf16[1024,768]{0,1:T(8,128)(2,1)}, bf16[1024,768]{0,1:T(8,128)(2,1)S(1)}, u32[]{:S(2)}) copy-start(bf16[1024,768]{0,1:T(8,128)(2,1)S(1)} %copy.140) | copy-start | bytes 4718596
  81.8 43.4 %copy-start.27 = (pred[512,512]{0,1:T(8,128)(4,1)}, pred[512,512]{0,1:T(8,128)(4,1)S(1)}, u32[]{:S(2)}) copy-start(pred[512,512]{0,1:T(8,128)(4,1)S(1)} %fusion.97) | copy-start | bytes 786436
  91.3 8.3 copy-start.19
  95.1 30.2 %copy-start.48 = (f32[12,512]{1,0:T(8,128)}, f32[12,512]{1,0:T(8,128)S(1)}, u32[]{:S(2)}) copy-start(f32[12,512]{1,0:T(8,128)S(1)} %get-tuple-element.156) | copy-start | bytes 73732
  99.6 25.7 %copy-start.52 = (f32[12,512]{1,0:T(8,128)}, f32[12,512]{1,0:T(8,128)S(1)}, u32[]{:S(2)}) copy-start(f32[12,512]{1,0:T(8,128)S(1)} %fusion.28) | copy-start | bytes 73732
  99.6 12.1 copy-start.20
  111.7 21.4 %copy-start.50 = (f32[12,512]{1,0:T(8,128)}, f32[12,512]{1,0:T(8,128)S(1)}, u32[]{:S(2)}) copy-start(f32[12,512]{1,0:T(8,128)S(1)} %get-tuple-element.154) | copy-start | bytes 73732
  111.7 13.6 %copy-start.33 = (bf16[1,512,768]{1,2,0:T(8,128)(2,1)S(1)}, bf16[1,512,768]{1,2,0:T(8,128)(2,1)}, u32[]{:S(2)}) copy-start(bf16[1,512,768]{1,2,0:T(8,128)(2,1)} %get-tuple-element.144) | copy-start | bytes 2359300
  111.7 21.4 %slice-start = ((s8[25165824]{0:T(1024)(128)(4,1)}), s8[4194304]{0:T(1024)(128)(4,1)S(1)}, s32[]{:S(2)}) async-start(s8[25165824]{0:T(1024)(128)(4,1)} %bitcast.262), calls=%async_computation.20 | async-start | bytes 8388608
  111.7 21.4 %slice-start.1 = ((s8[25165824]{0:T(1024)(128)(4,1)}), s8[4194304]{0:T(1024)(128)(4,1)S(1)}, s32[]{:S(2)}) async-start(s8[25165824]{0:T(1024)(128)(4,1)} %bitcast.262), calls=%async_computation.21 | async-start | bytes 8388608
  125.3 7.8 copy-start.54
  125.3 7.8 slice-start.2
  125.3 7.8 slice-start.3
  125.3 8.6 slice-start.4
  125.3 9.8 slice-start.5
  125.3 10.2 copy-start.29
  150.7 11.6 copy-start.17
  185.2 109.2 %all-to-all-start = ((bf16[8,4,96,768]{3,2,1,0:T(8,128)(2,1)}), bf16[8,4,96,768]{3,2,1,0:T(8,128)(2,1)}, u32[]{:S(2)}, u32[]{:S(2)}) async-start(bf16[8,4,96,768]{3,2,1,0:T(8,128)(2,1)} %bitcast.269), calls=%async_computation | async-start | bytes 9437184 | tf_op jit(solution)/shard_map/all_to_all | solution.py:216
  190.6 202.5 %all-gather.13.cloned.1.call-start = ((), (), s32[]{:S(2)}) async-start(), calls=%async_computation.12 | async-start | bytes 11796480 | tf_op jit(solution)/shard_map/all_gather | solution.py:181
  298.8 16.5 %copy-start.35 = (bf16[8,2,1,96,768]{4,3,2,1,0:T(8,128)(2,1)}, bf16[8,2,1,96,768]{4,3,2,1,0:T(8,128)(2,1)S(1)}, u32[]{:S(2)}) copy-start(bf16[8,2,1,96,768]{4,3,2,1,0:T(8,128)(2,1)S(1)} %get-tuple-element.139) | copy-start | bytes 7077892
  414.7 170.1 %all-to-all-start.1 = ((bf16[8,4,96,768]{3,2,1,0:T(8,128)(2,1)}), bf16[8,4,96,768]{3,2,1,0:T(8,128)(2,1)}, u32[]{:S(2)}, u32[]{:S(2)}) async-start(bf16[8,4,96,768]{3,2,1,0:T(8,128)(2,1)} %bitcast.268), calls=%async_computation.1 | async-start | bytes 9437184 | tf_op jit(solution)/shard_map/all_to_all | solution.py:225
  420.3 790.3 %reduce-scatter.14.cloned.1.call-start = ((), (), s32[]{:S(2)}) async-start(), calls=%async_computation.18 | async-start | bytes 11796480 | tf_op jit(solution)/shard_map/reduce_scatter | solution.py:309
  420.7 183.6 %copy-start.46 = (pred[1024,2]{1,0:T(8,128)(4,1)}, pred[1024,2]{1,0:T(8,128)(4,1)S(1)}, u32[]{:S(2)}) copy-start(pred[1024,2]{1,0:T(8,128)(4,1)S(1)} %copy.153) | copy-start | bytes 6148
  432.7 152.0 %copy-start.57 = (s32[1024,2]{0,1:T(2,128)S(1)}, s32[1024,2]{0,1:T(2,128)}, u32[]{:S(2)}) copy-start(s32[1024,2]{0,1:T(2,128)} %param.31) | copy-start | bytes 24580
  581.5 16.7 %copy-start.2 = (s32[2048]{0:T(1024)}, s32[2048]{0:T(1024)S(1)}, u32[]{:S(2)}) copy-start(s32[2048]{0:T(1024)S(1)} %broadcast_clamp_fusion) | copy-start | bytes 24580
  584.7 37.6 %copy-start.95 = (f32[1024]{0:T(1024)}, f32[1024]{0:T(1024)S(1)}, u32[]{:S(2)}) copy-start(f32[1024]{0:T(1024)S(1)} %get-tuple-element.123) | copy-start | bytes 12292
  604.3 40.0 %copy-start.10 = (bf16[1024,2,768]{2,1,0:T(2,128)(2,1)}, bf16[1024,2,768]{2,1,0:T(2,128)(2,1)S(1)}, u32[]{:S(2)}) copy-start(bf16[1024,2,768]{2,1,0:T(2,128)(2,1)S(1)} %reshape.648) | copy-start | bytes 9437188
  604.3 18.1 %copy-start.60 = (s32[1024,2]{0,1:T(2,128)S(1)}, s32[1024,2]{0,1:T(2,128)}, u32[]{:S(2)}) copy-start(s32[1024,2]{0,1:T(2,128)} %copy-done.59) | copy-start | bytes 24580
  604.3 18.1 %copy-start.85 = (pred[1024]{0:T(1024)(128)(4,1)S(1)}, pred[1024]{0:T(1024)(128)(4,1)}, u32[]{:S(2)}) copy-start(pred[1024]{0:T(1024)(128)(4,1)} %copy-done.84) | copy-start | bytes 3076
  604.3 21.1 %copy-start.69 = (s32[2048]{0:T(1024)S(1)}, s32[2048]{0:T(1024)}, u32[]{:S(2)}) copy-start(s32[2048]{0:T(1024)} %copy-done.68) | copy-start | bytes 24580
  604.3 21.1 %copy-start.99 = (pred[2048]{0:T(1024)(128)(4,1)S(1)}, pred[2048]{0:T(1024)(128)(4,1)}, u32[]{:S(2)}) copy-start(pred[2048]{0:T(1024)(128)(4,1)} %copy-done.98) | copy-start | bytes 6148
  622.4 21.9 %copy-start.70 = (f32[1024,2]{0,1:T(2,128)}, f32[1024,2]{0,1:T(2,128)S(1)}, u32[]{:S(2)}) copy-start(f32[1024,2]{0,1:T(2,128)S(1)} %copy.193) | copy-start | bytes 24580
  623.0 21.3 %copy-start.72 = (f32[1024,2]{0,1:T(2,128)}, f32[1024,2]{0,1:T(2,128)S(1)}, u32[]{:S(2)}) copy-start(f32[1024,2]{0,1:T(2,128)S(1)} %get-tuple-element.134) | copy-start | bytes 24580
  769.0 26.1 %copy-start.36 = (bf16[8,2,1,96,768]{4,3,2,1,0:T(8,128)(2,1)S(1)}, bf16[8,2,1,96,768]{4,3,2,1,0:T(8,128)(2,1)}, u32[]{:S(2)}) copy-start(bf16[8,2,1,96,768]{4,3,2,1,0:T(8,128)(2,1)} %copy-done.35) | copy-start | bytes 7077892
  769.0 445.9 %reduce-scatter.12.cloned.1.call-start = ((), (), s32[]{:S(2)}) async-start(), calls=%async_computation.17 | async-start | bytes 11796480 | tf_op jit(solution)/shard_map/reduce_scatter | solution.py:306
  806.9 14.6 %copy-start.110 = (bf16[8,2,96,3072]{3,2,0,1:T(8,128)(2,1)S(1)}, bf16[8,2,96,3072]{3,2,0,1:T(8,128)(2,1)}, u32[]{:S(2)}) copy-start(bf16[8,2,96,3072]{3,2,0,1:T(8,128)(2,1)} %copy-done.109) | copy-start | bytes 28311556
  863.0 108.3 %copy-start.3 = (s32[2048]{0:T(1024)S(1)}, s32[2048]{0:T(1024)}, u32[]{:S(2)}) copy-start(s32[2048]{0:T(1024)} %copy-done.2) | copy-start | bytes 24580
  863.0 108.3 %all-to-all-start.3 = ((bf16[8,4,96,768]{3,2,1,0:T(8,128)(2,1)}), bf16[8,4,96,768]{3,2,1,0:T(8,128)(2,1)}, u32[]{:S(2)}, u32[]{:S(2)}) async-start(bf16[8,4,96,768]{3,2,1,0:T(8,128)(2,1)} %bitcast.267), calls=%async_computation.3 | async-start | bytes 9437184 | tf_op jit(solution)/shard_map/all_to_all | solution.py:265
  867.9 351.3 %reduce-scatter.16.cloned.1.call-start = ((), (), s32[]{:S(2)}) async-start(), calls=%async_computation.19 | async-start | bytes 405504
  870.7 348.5 %reduce-scatter.10.cloned.1.call-start = ((), (), s32[]{:S(2)}) async-start(), calls=%async_computation.16 | async-start | bytes 2433024 | tf_op jit(solution)/shard_map/reduce_scatter | solution.py:301
  984.8 7.4 copy-start.11
  984.8 7.4 copy-start.47
  1027.1 9.3 slice-start.6
  1027.1 9.3 slice-start.7
  1068.1 13.4 %copy-start.5 = (f32[12,512,512]{1,2,0:T(8,128)S(1)}, f32[12,512,512]{1,2,0:T(8,128)}, u32[]{:S(2)}) copy-start(f32[12,512,512]{1,2,0:T(8,128)} %get-tuple-element.164) | copy-start | bytes 37748740
  1098.3 223.8 %reduce-scatter.8.cloned.1.call-start = ((), (), s32[]{:S(2)}) async-start(), calls=%async_computation.15 | async-start | bytes 7299072 | tf_op jit(solution)/shard_map/reduce_scatter | solution.py:300
  1116.3 7.5 copy-start.1
  1131.3 8.8 copy-start.9
  1131.3 8.8 copy-start.79
  1131.3 8.8 copy-start.88
  1131.3 8.8 copy-start.90
  1159.8 42.6 %copy-start.16 = (bf16[1024,768]{0,1:T(8,128)(2,1)S(1)}, bf16[1024,768]{0,1:T(8,128)(2,1)}, u32[]{:S(2)}) copy-start(bf16[1024,768]{0,1:T(8,128)(2,1)} %copy-done.14) | copy-start | bytes 4718596
  (71 other events, 265.0 us)
Sparse Core Ops, SparseCore 0:
  11.5 63.2 all-gather.6
  78.3 52.9 all-gather.8
  132.9 63.0 all-gather.14
  197.4 64.3 all-gather.10
  263.1 64.2 all-gather.16
  328.8 64.2 all-gather.12
  769.1 76.6 reduce-scatter.13
  848.4 77.7 reduce-scatter.11
  931.7 95.5 reduce-scatter.15
  1098.4 98.9 reduce-scatter.9
  1203.6 118.3 reduce-scatter.7
where the time goes:
time: 1340 us; the launch traced here: 1330 us
  waiting for transfers between devices  351 us (26%)
  blocking collectives  326 us (24%)
  matrix products  296 us (22%)
  other arithmetic  180 us (13%)
  local copies, waits for them, and re-layouts  144 us (11%)
  starting transfers between devices  16.3 us (1%)
  between operations  15.9 us (1%)
    all_gather x1, blocking collectives, local(): lax.all_gather(router.astype(jnp.bfloat16), ('dp', 'expert'), axis=0, til...  140 us
    all_to_all x1, blocking collectives, local(): lax.all_to_all(d_send, 'expert', split_axis=0, concat_axis=0, tiled=True)  105 us
    reduce_scatter x1, waiting for transfers between devices, local(): lax.psum_scatter(grad_projections, ('dp', 'expert'), scatter_dimension=0,...  103 us
    all_to_all x1, waiting for transfers between devices, local(): lax.all_to_all(d_expert_in, 'expert', split_axis=0, concat_axis=0, tiled=...  101 us
    all_to_all x1, waiting for transfers between devices, local(): lax.all_to_all(send_rows, 'expert', split_axis=0, concat_axis=0, tiled=True)  99.8 us
    unnamed x2, blocking collectives  81.1 us
    all_gather x1, waiting for transfers between devices, local(): lax.all_gather(train_out.astype(jnp.bfloat16), 'dp', axis=2, tiled=True)  47.5 us
    dot_general x2, matrix products, expert_inner_grad(): jnp.einsum('nlcd,ldf->nlcf', d_rows, weight_out, preferred_element_type=j...  37.1 us
  transfers between devices with their start and end apart: 14, of which 4 were waited for; matrix products, arithmetic and copies ran while one was open for 37% of the time, Pallas kernels for 0%

commit v1 on v0

v1 whole, which is shorter than its diff:
```python
import functools

import jax
import jax.numpy as jnp
from jax import lax
from jax.experimental import pallas as pl
from jax.experimental.pallas import tpu as pltpu
from jax.sharding import PartitionSpec as P

HD = 64
CAP = 96
EXTRA = 16

epsilon = 1e-05
masked_score = -1e30
F32 = jnp.float32
BF = jnp.bfloat16


def layer_norm(values):
    centre = jnp.mean(values, axis=-1, keepdims=True)
    centred = values - centre
    spread = jnp.mean(centred * centred, axis=-1, keepdims=True)
    return centred * lax.rsqrt(spread + epsilon)


def seen_pairs(seg_ids, valid_ids, row_start, row_stop):
    rows_here = jnp.arange(row_start, row_stop, dtype=jnp.int32)[:, None]
    keys_here = jnp.arange(row_stop, dtype=jnp.int32)[None, :]
    same_segment = seg_ids[row_start:row_stop, None] == seg_ids[None, :row_stop]
    return same_segment & (keys_here <= rows_here) & (valid_ids[None, :row_stop] > 0)


def attend_forward(query, key_rows, value_rows, seg_ids, valid_ids, head_count):
    row_count = query.shape[0]
    block_rows = min(512, row_count)
    scale = HD ** (-0.5)
    out_blocks = []
    log_sums = []
    for row_start in range(0, row_count, block_rows):
        row_stop = row_start + block_rows
        query_head = query[row_start:row_stop].reshape(block_rows, head_count, HD)
        key_head = key_rows[:row_stop].reshape(row_stop, head_count, HD)
        value_head = value_rows[:row_stop].reshape(row_stop, head_count, HD)
        scores = (
            jnp.einsum("qhd,khd->hqk", query_head, key_head, preferred_element_type=jnp.float32)
            * scale
        )
        scores = jnp.where(
            seen_pairs(seg_ids, valid_ids, row_start, row_stop)[None], scores, masked_score
        )
        row_max = jnp.max(scores, axis=-1, keepdims=True)
        exponent = jnp.exp(scores - row_max)
        row_total = jnp.sum(exponent, axis=-1, keepdims=True)
        attention = (exponent / row_total).astype(jnp.bfloat16)
        combined = jnp.einsum(
            "hqk,khd->qhd", attention, value_head, preferred_element_type=jnp.float32
        )
        out_blocks.append(combined.reshape(block_rows, head_count * HD).astype(jnp.bfloat16))
        log_sums.append(row_max + jnp.log(row_total))
    return (jnp.concatenate(out_blocks, axis=0), log_sums)


def attend_backward(query, key_rows, value_rows, d_heads, seg_ids, valid_ids, log_sums, head_count):
    row_count = query.shape[0]
    block_rows = min(512, row_count)
    scale = HD ** (-0.5)
    d_query_blocks = []
    d_key = jnp.zeros((row_count, head_count, HD), jnp.float32)
    d_value = jnp.zeros((row_count, head_count, HD), jnp.float32)
    for block_number, row_start in enumerate(range(0, row_count, block_rows)):
        row_stop = row_start + block_rows
        query_head = query[row_start:row_stop].reshape(block_rows, head_count, HD)
        key_head = key_rows[:row_stop].reshape(row_stop, head_count, HD)
        value_head = value_rows[:row_stop].reshape(row_stop, head_count, HD)
        grad_head = d_heads[row_start:row_stop].reshape(block_rows, head_count, HD)
        scores = (
            jnp.einsum("qhd,khd->hqk", query_head, key_head, preferred_element_type=jnp.float32)
            * scale
        )
        scores = jnp.where(
            seen_pairs(seg_ids, valid_ids, row_start, row_stop)[None], scores, masked_score
        )
        attention = jnp.exp(scores - log_sums[block_number])
        d_attention = jnp.einsum(
            "qhd,khd->hqk", grad_head, value_head, preferred_element_type=jnp.float32
        )
        d_scores = (
            attention * (d_attention - jnp.sum(d_attention * attention, axis=-1, keepdims=True))
        ).astype(jnp.bfloat16)
        d_query_blocks.append(
            (
                jnp.einsum("hqk,khd->qhd", d_scores, key_head, preferred_element_type=jnp.float32)
                * scale
            ).reshape(block_rows, head_count * HD)
        )
        d_key = d_key.at[:row_stop].add(
            jnp.einsum("hqk,qhd->khd", d_scores, query_head, preferred_element_type=jnp.float32)
            * scale
        )
        d_value = d_value.at[:row_stop].add(
            jnp.einsum(
                "hqk,qhd->khd",
                attention.astype(jnp.bfloat16),
                grad_head,
                preferred_element_type=jnp.float32,
            )
        )
    d_query = jnp.concatenate(d_query_blocks, axis=0).astype(jnp.bfloat16)
    return (
        d_query,
        d_key.reshape(row_count, head_count * HD).astype(jnp.bfloat16),
        d_value.reshape(row_count, head_count * HD).astype(jnp.bfloat16),
    )


def iota(shape, axis):
    return lax.broadcasted_iota(jnp.int32, shape, axis)


def dot(a, b):
    return jnp.dot(a, b, preferred_element_type=F32)


def dot_nt(a, b):
    return lax.dot_general(a, b, (((1,), (1,)), ((), ())), preferred_element_type=F32)


def lanes_up(count):
    return -(-count // 128) * 128


def cost(flops, nbytes):
    return pl.CostEstimate(flops=int(flops), bytes_accessed=int(nbytes), transcendentals=0)


def whole(shape):
    zeros = (0,) * len(shape)
    return pl.BlockSpec(shape, lambda *_: zeros)


def dispatch_rows(group, slot_ref, rows_ref, a_ref, b_ref, local_count):
    half = local_count // 2
    tokens = rows_ref.shape[0]
    slots = iota((CAP, tokens), 0)
    picks = []
    for c in range(2):
        for i in range(half):
            row = slot_ref[pl.ds(group * local_count + 2 * i + c, 1), :]
            picks.append((row == slots).astype(F32).astype(BF))
    chosen = jnp.concatenate(picks, axis=0)
    moved = dot(chosen, rows_ref[...]).astype(BF)
    a_ref[0, : half * CAP, :] = moved[: half * CAP]
    b_ref[0, : half * CAP, :] = moved[half * CAP :]
    return chosen


def first_dispatch_kernel(
    routes_ref, routes_t_ref, valid_ref, valid_t_ref, rows_ref,
    slot_ref, dest_ref, a_ref, b_ref, *, expert_count, local_count,
):
    group = pl.program_id(0)
    tokens = rows_ref.shape[0]
    half = local_count // 2

    @pl.when(group == 0)
    def _():
        row_ids = iota((tokens, tokens), 0)
        col_ids = iota((tokens, tokens), 1)
        experts_t = iota((expert_count, tokens), 0)
        live_t = (
            (routes_t_ref[0:1, :] == experts_t) | (routes_t_ref[1:2, :] == experts_t)
        ) & (valid_t_ref[...] > 0)
        above = (row_ids < col_ids).astype(F32).astype(BF)
        earlier_t = dot(live_t.astype(F32).astype(BF), above)
        slot_ref[...] = jnp.where(
            live_t & (earlier_t < CAP), earlier_t, -1.0
        ).astype(jnp.int32)

        experts = iota((tokens, expert_count), 1)
        first = routes_ref[:, 0:1]
        second = routes_ref[:, 1:2]
        live = ((first == experts) | (second == experts)) & (valid_ref[...] > 0)
        below = (col_ids < row_ids).astype(F32).astype(BF)
        earlier = dot(below, live.astype(F32).astype(BF))
        kept = jnp.where(live & (earlier < CAP), earlier, -1.0)
        lanes = iota((tokens, 128), 1)
        table = jnp.full((tokens, 128), -1, jnp.int32)
        bits = local_count.bit_length() - 1
        for k, route in enumerate((first, second)):
            slot = jnp.sum(
                jnp.where(route == experts, kept, 0.0), axis=1, keepdims=True
            ).astype(jnp.int32)
            place = lax.shift_right_logical(route, bits)
            inner = lax.shift_right_logical(route & (local_count - 1), 1)
            for stride, base in ((half * CAP + EXTRA, 0), (half * CAP, 4)):
                code = place * stride + inner * CAP + slot
                for c in range(2):
                    ok = (slot >= 0) & ((route & 1) == c)
                    table = jnp.where(
                        lanes == base + 2 * c + k, jnp.where(ok, code, -1), table
                    )
        dest_ref[...] = table

    dispatch_rows(group, slot_ref, rows_ref, a_ref, b_ref, local_count)


def first_dispatch(routes, valid, rows, expert_count, groups):
    tokens, width = rows.shape
    local_count = expert_count // groups
    block = (local_count // 2) * CAP
    out_spec = pl.BlockSpec((1, block, width), lambda g: (g, 0, 0))
    return pl.pallas_call(
        functools.partial(
            first_dispatch_kernel, expert_count=expert_count, local_count=local_count
        ),
        name="first_dispatch",
        grid=(groups,),
        in_specs=[
            whole((tokens, 2)), whole((2, tokens)), whole((tokens, 1)), whole((1, tokens)),
            whole((tokens, width)),
        ],
        out_specs=[whole((expert_count, tokens)), whole((tokens, 128)), out_spec, out_spec],
        out_shape=[
            jax.ShapeDtypeStruct((expert_count, tokens), jnp.int32),
            jax.ShapeDtypeStruct((tokens, 128), jnp.int32),
            jax.ShapeDtypeStruct((groups, block, width), BF),
            jax.ShapeDtypeStruct((groups, block, width), BF),
        ],
        cost_estimate=cost(2 * expert_count * CAP * tokens * width, 8e6),
    )(routes, routes.T, valid[:, None], valid[None, :], rows)


def split_two(values):
    high = values.astype(BF).astype(F32)
    return high, values - high


def second_dispatch_kernel(slot_ref, gate_ref, rows_ref, a_ref, b_ref, *, local_count):
    group = pl.program_id(0)
    half = local_count // 2
    total = local_count * CAP
    block = half * CAP
    width = rows_ref.shape[1]
    chosen = dispatch_rows(group, slot_ref, rows_ref, a_ref, b_ref, local_count)
    high, low = split_two(gate_ref[...])
    experts = gate_ref.shape[0]
    every = dot_nt(jnp.concatenate([high.astype(BF), low.astype(BF)], axis=0), chosen)
    column = iota((experts, total), 1)
    expert = iota((experts, total), 0)
    mine = jnp.zeros((experts, total), jnp.bool_)
    for c in range(2):
        for i in range(half):
            start = (c * half + i) * CAP
            mine = mine | (
                (column >= start)
                & (column < start + CAP)
                & (expert == group * local_count + 2 * i + c)
            )
    high_row = jnp.sum(jnp.where(mine, every[:experts], 0.0), axis=0, keepdims=True)
    low_row = jnp.sum(jnp.where(mine, every[experts:], 0.0), axis=0, keepdims=True)
    sub = iota((EXTRA, total), 0)
    tail = jnp.where(sub == 0, high_row, jnp.where(sub == 1, low_row, 0.0)).astype(BF)
    for ref in (a_ref, b_ref):
        ref[0, block:, :] = jnp.zeros((EXTRA, width), BF)
        ref[0, block:, :total] = tail


def second_dispatch(slot_table, gate_t, rows, groups):
    tokens, width = rows.shape
    expert_count = slot_table.shape[0]
    local_count = expert_count // groups
    block = (local_count // 2) * CAP + EXTRA
    out_spec = pl.BlockSpec((1, block, width), lambda g: (g, 0, 0))
    return pl.pallas_call(
        functools.partial(second_dispatch_kernel, local_count=local_count),
        name="second_dispatch",
        grid=(groups,),
        in_specs=[
            whole((expert_count, tokens)), whole((expert_count, tokens)), whole((tokens, width)),
        ],
        out_specs=[out_spec, out_spec],
        out_shape=[jax.ShapeDtypeStruct((groups, block, width), BF)] * 2,
        cost_estimate=cost(2 * expert_count * CAP * tokens * width, 8e6),
    )(slot_table, gate_t, rows)


GELU_SLOPE = 0.7978845608028654
GELU_CUBE = 0.044715


def expert_kernel(*refs, train, chunk, half, groups, row_block):
    if train:
        x_ref, t_ref, u_ref, v_ref, y_ref, dx_ref, gu_ref, gv_ref = refs[:8]
        xs, dys, gate_s, y_acc, dx_acc, c_s, dz_s, x_t, dy_t = refs[8:]
    else:
        x_ref, t_ref, u_ref, v_ref, y_ref, dx_ref = refs[:6]
        xs, dys, gate_s, y_acc, dx_acc = refs[6:]
    i = pl.program_id(0)
    f = pl.program_id(1)
    block = half * CAP
    width = xs.shape[1]
    rows = groups * CAP
    mine = pl.ds(pl.multiple_of(i * CAP, CAP), CAP)

    @pl.when((i == 0) & (f == 0))
    def _():
        dx_ref[:, block:, :] = jnp.zeros((groups, EXTRA, width), BF)

    @pl.when(f == 0)
    def _():
        wide = lanes_up(2 * block)
        lane = iota((CAP, wide), 1)
        sub = iota((CAP, wide), 0)
        hit = lane == sub + (chunk * half + i) * CAP
        for g in range(groups):
            at = slice(g * CAP, (g + 1) * CAP)
            gates = jnp.sum(
                x_ref[g, block:, :wide].astype(F32), axis=0, keepdims=True
            )
            gate = jnp.sum(jnp.where(hit, gates, 0.0), axis=1, keepdims=True)
            gate_s[at, :] = jnp.broadcast_to(gate, (CAP, 128))
            x = x_ref[g, mine, :]
            xs[at, :] = x
            dy = (gate * t_ref[g, mine, :].astype(F32)).astype(BF)
            dys[at, :] = dy
        y_acc[...] = jnp.zeros((rows, width), F32)
        dx_acc[...] = jnp.zeros((rows, width), F32)
        if train:
            x_t[...] = xs[...].T
            dy_t[...] = dys[...].T

    @pl.loop(0, rows // row_block)
    def _(b):
        at = pl.ds(pl.multiple_of(b * row_block, row_block), row_block)
        u = u_ref[0, 0]
        v = v_ref[0, 0]
        z = dot(xs[at, :], u)
        dc = dot(dys[at, :], v)
        square = z * z
        bend = jnp.tanh(GELU_SLOPE * z * (1.0 + GELU_CUBE * square))
        half_up = 0.5 + 0.5 * bend
        c = (z * half_up).astype(BF)
        slope = half_up + (0.5 * GELU_SLOPE) * z * (1.0 - bend * bend) * (
            1.0 + (3.0 * GELU_CUBE) * square
        )
        dz = (dc * slope).astype(BF)
        y_acc[at, :] += dot_nt(c, v)
        dx_acc[at, :] += dot_nt(dz, u)
        if train:
            c_s[at, :] = c
            dz_s[at, :] = dz

    if train:
        step = min(256, width)

        @pl.loop(0, width // step)
        def _(b):
            at = pl.ds(pl.multiple_of(b * step, step), step)
            gu_ref[0, 0, at, :] = dot(x_t[at, :], dz_s[...]).astype(BF)
            gv_ref[0, 0, at, :] = dot(dy_t[at, :], c_s[...]).astype(BF)

    @pl.when(f == pl.num_programs(1) - 1)
    def _():
        wide = lanes_up(block)
        lane = iota((CAP, wide), 1)
        sub = iota((CAP, wide), 0)
        hit = lane == sub + i * CAP
        tail_sub = iota((EXTRA, wide), 0)
        for g in range(groups):
            at = slice(g * CAP, (g + 1) * CAP)
            y = y_acc[at, :].astype(BF).astype(F32)
            d_gate = jnp.sum(t_ref[g, mine, :].astype(F32) * y, axis=1, keepdims=True)
            row = jnp.sum(jnp.where(hit, d_gate, 0.0), axis=0, keepdims=True)
            high, low = split_two(row)
            tail = jnp.where(tail_sub == 0, high, jnp.where(tail_sub == 1, low, 0.0))
            dx_ref[g, block:, :wide] = (
                dx_ref[g, block:, :wide].astype(F32) + tail
            ).astype(BF)
            y_ref[g, mine, :] = (gate_s[at, 0:1] * y).astype(BF)
            dx_ref[g, mine, :] = dx_acc[at, :].astype(BF)


def run_experts(x_rows, t_rows, weight_in, weight_out, chunk, train):
    groups, x_block, width = x_rows.shape
    block = x_block - EXTRA
    parts, half, _, hidden = weight_in.shape
    rows = groups * CAP
    weight_spec = pl.BlockSpec((1, 1, width, hidden), lambda i, f: (f, i, 0, 0))
    out_specs = [whole((groups, block, width)), whole((groups, x_block, width))]
    out_shape = [
        jax.ShapeDtypeStruct((groups, block, width), BF),
        jax.ShapeDtypeStruct((groups, x_block, width), BF),
    ]
    scratch = [
        pltpu.VMEM((rows, width), BF), pltpu.VMEM((rows, width), BF),
        pltpu.VMEM((rows, 128), F32),
        pltpu.VMEM((rows, width), F32), pltpu.VMEM((rows, width), F32),
    ]
    if train:
        out_specs += [weight_spec, weight_spec]
        out_shape += [jax.ShapeDtypeStruct(weight_in.shape, BF)] * 2
        scratch += [
            pltpu.VMEM((rows, hidden), BF), pltpu.VMEM((rows, hidden), BF),
            pltpu.VMEM((width, rows), BF), pltpu.VMEM((width, rows), BF),
        ]
    products = 6 if train else 4
    return pl.pallas_call(
        functools.partial(
            expert_kernel, train=train, chunk=chunk, half=half, groups=groups,
            row_block=min(256, rows),
        ),
        name="experts_train" if train else "experts_frozen",
        grid=(half, parts),
        in_specs=[
            whole((groups, x_block, width)), whole((groups, block, width)),
            weight_spec, weight_spec,
        ],
        out_specs=out_specs,
        out_shape=out_shape,
        scratch_shapes=scratch,
        cost_estimate=cost(products * 2 * half * rows * width * hidden * parts, 30e6),
    )(x_rows, t_rows, weight_in, weight_out)


def two_hot(dest, column, count):
    place = iota((dest.shape[0], count), 1)
    hit = (dest[:, column : column + 1] == place) | (dest[:, column + 1 : column + 2] == place)
    return hit.astype(F32).astype(BF)


def combine_back_kernel(dest_ref, a_ref, b_ref, rows_ref, gate_ref, table, *, half, groups):
    stride = half * CAP + EXTRA
    block = half * CAP
    count = groups * stride

    @pl.when(pl.program_id(0) == 0)
    def _():
        wide = lanes_up(block)
        eye = iota((block, wide), 0) == iota((block, wide), 1)
        lane = iota((block, 128), 1)
        inner = iota((block, 128), 0) // CAP if half > 1 else jnp.zeros((block, 128), jnp.int32)
        for c, ref in enumerate((a_ref, b_ref)):
            for g in range(groups):
                tail = ref[g * stride + block : (g + 1) * stride, :wide].astype(F32)
                high = jnp.sum(jnp.where(eye, tail[0:1, :], 0.0), axis=1, keepdims=True)
                low = jnp.sum(jnp.where(eye, tail[1:2, :], 0.0), axis=1, keepdims=True)
                spot = 2 * (g * half + inner) + c
                table[c, g * stride : g * stride + block, :] = jnp.where(
                    lane == spot, high, jnp.where(lane == spot + 64, low, 0.0)
                ).astype(BF)
                table[c, g * stride + block : (g + 1) * stride, :] = jnp.zeros((EXTRA, 128), BF)

    dest = dest_ref[...]
    hot_a = two_hot(dest, 0, count)
    hot_b = two_hot(dest, 2, count)
    rows_ref[...] = dot(hot_a, a_ref[...]) + dot(hot_b, b_ref[...])
    gate_ref[...] = dot(hot_a, table[0]) + dot(hot_b, table[1])


def combine_back(dest, rows_a, rows_b, half, groups):
    tokens = dest.shape[0]
    width = rows_a.shape[-1]
    count = groups * (half * CAP + EXTRA)
    step = min(256, tokens)
    row_spec = pl.BlockSpec((step, width), lambda b: (b, 0))
    lane_spec = pl.BlockSpec((step, 128), lambda b: (b, 0))
    return pl.pallas_call(
        functools.partial(combine_back_kernel, half=half, groups=groups),
        name="combine_back",
        grid=(tokens // step,),
        in_specs=[lane_spec, whole((count, width)), whole((count, width))],
        out_specs=[row_spec, lane_spec],
        out_shape=[
            jax.ShapeDtypeStruct((tokens, width), F32),
            jax.ShapeDtypeStruct((tokens, 128), F32),
        ],
        scratch_shapes=[pltpu.VMEM((2, count, 128), BF)],
        cost_estimate=cost(4 * tokens * count * width, 12e6),
    )(dest, rows_a.reshape(count, width), rows_b.reshape(count, width))


def combine_out_kernel(dest_ref, a_ref, b_ref, resid_ref, valid_ref, out_ref):
    count = a_ref.shape[0]
    dest = dest_ref[...]
    mixed = dot(two_hot(dest, 4, count), a_ref[...]) + dot(two_hot(dest, 6, count), b_ref[...])
    out_ref[...] = ((resid_ref[...] + mixed) * valid_ref[...].astype(F32)).astype(BF)


def combine_out(dest, rows_a, rows_b, resid, valid):
    tokens, width = resid.shape
    count = rows_a.shape[0] * rows_a.shape[1]
    step = min(256, tokens)
    return pl.pallas_call(
        combine_out_kernel,
        name="combine_out",
        grid=(tokens // step,),
        in_specs=[
            pl.BlockSpec((step, 128), lambda b: (b, 0)),
            whole((count, width)), whole((count, width)),
            pl.BlockSpec((step, width), lambda b: (b, 0)),
            pl.BlockSpec((step, 1), lambda b: (b, 0)),
        ],
        out_specs=pl.BlockSpec((step, width), lambda b: (b, 0)),
        out_shape=jax.ShapeDtypeStruct((tokens, width), BF),
        cost_estimate=cost(4 * tokens * count * width, 12e6),
    )(dest, rows_a.reshape(count, width), rows_b.reshape(count, width), resid, valid[:, None])


def pad_to(values, count):
    return jnp.pad(values, [(0, 0)] * (values.ndim - 1) + [(0, count - values.shape[-1])])


def swap(rows):
    return lax.all_to_all(rows, "expert", split_axis=0, concat_axis=0, tiled=True)


BOTH = ("dp", "expert")


def local(
    tokens,
    segment,
    valid,
    routes,
    out_grad,
    norm1_gain,
    qkv_weight,
    out_weight,
    norm2_gain,
    router,
    train_in,
    train_out,
    frozen_in,
    frozen_out,
):
    token_count, width = tokens.shape
    head_count = width // HD
    expert_count = router.shape[1]
    groups = lax.axis_size("expert")
    devices = groups * lax.axis_size("dp")
    local_count = expert_count // groups
    half = local_count // 2

    small = jnp.concatenate([router.reshape(-1), norm1_gain, norm2_gain])
    small_rows = -(-small.shape[0] // width)
    small = pad_to(small[None], small_rows * width).reshape(small_rows, width)
    payload = jnp.concatenate([qkv_weight, out_weight, small], axis=0).astype(BF)
    dense = lax.all_gather(payload, BOTH, axis=0, tiled=False)
    q_rows, o_rows, gain_rows = qkv_weight.shape[0], out_weight.shape[0], norm1_gain.shape[0]
    projection_stack = dense[:, :q_rows].reshape(3, width, width)
    attention_out = dense[:, q_rows : q_rows + o_rows].reshape(width, width)
    tail = dense[:, q_rows + o_rows :].reshape(devices, small_rows * width)
    router_size = gain_rows * expert_count
    router_low = tail[:, :router_size].reshape(width, expert_count)
    gain_one = tail[:, router_size : router_size + gain_rows].reshape(width).astype(F32)
    gain_two = (
        tail[:, router_size + gain_rows : router_size + 2 * gain_rows]
        .reshape(width)
        .astype(F32)
    )

    slot_table, dest, t_send_a, t_send_b = first_dispatch(
        routes, valid, out_grad, expert_count, groups
    )
    t_a = swap(t_send_a)
    t_b = swap(t_send_b)

    experts_low = [
        lax.all_gather(w.astype(BF), "dp", axis=0, tiled=False)
        for w in (train_in, train_out, frozen_in, frozen_out)
    ]

    tokens_f = tokens.astype(F32)
    valid_f = valid.astype(F32)[:, None]
    norm_one = layer_norm(tokens_f)
    act = (norm_one * gain_one).astype(BF)
    projected = jnp.einsum(
        "td,jde->jte", act, projection_stack, preferred_element_type=F32
    ).astype(BF)
    query, key_rows, value_rows = (projected[0], projected[1], projected[2])
    heads_out, log_sums = attend_forward(query, key_rows, value_rows, segment, valid, head_count)
    attn = jnp.dot(heads_out, attention_out, preferred_element_type=F32) * valid_f
    resid = tokens_f + attn
    norm_two = layer_norm(resid)
    hidden = (norm_two * gain_two).astype(BF)
    logits = jnp.dot(hidden, router_low, preferred_element_type=F32)
    soft = jax.nn.softmax(logits, axis=-1)
    expert_ids = jnp.arange(expert_count, dtype=jnp.int32)[None, :]
    choose = ((routes[:, 0:1] == expert_ids) | (routes[:, 1:2] == expert_ids)).astype(F32)
    picked = soft * choose
    picked_total = jnp.sum(picked, axis=1, keepdims=True)
    gates = picked / picked_total

    x_send_a, x_send_b = second_dispatch(slot_table, gates.T, hidden, groups)
    x_a = swap(x_send_a)
    x_b = swap(x_send_b)
    y_a, dx_a, grad_in, grad_out = run_experts(
        x_a, t_a, experts_low[0], experts_low[1], 0, True
    )
    dx_a = swap(dx_a)
    y_b, dx_b = run_experts(x_b, t_b, experts_low[2], experts_low[3], 1, False)
    dx_b = swap(dx_b)
    y_a = swap(y_a)
    y_b = swap(y_b)
    grad_train_in = lax.psum_scatter(grad_in, "dp", scatter_dimension=0, tiled=False).astype(F32)
    grad_train_out = lax.psum_scatter(grad_out, "dp", scatter_dimension=0, tiled=False).astype(
        F32
    )
    output = combine_out(dest, y_a, y_b, resid, valid)

    d_hidden, gate_parts = combine_back(dest, dx_a, dx_b, half, groups)
    cotangent = out_grad.astype(F32) * valid_f
    d_gate = gate_parts[:, :expert_count] + gate_parts[:, 64 : 64 + expert_count]
    d_picked = choose * (d_gate - jnp.sum(d_gate * gates, axis=1, keepdims=True)) / picked_total
    d_logits = (soft * (d_picked - jnp.sum(d_picked * soft, axis=-1, keepdims=True))).astype(BF)
    grad_router = jnp.dot(hidden.T, d_logits, preferred_element_type=F32)
    d_hidden = d_hidden + jnp.dot(d_logits, router_low.T, preferred_element_type=F32)
    grad_gain_two = jnp.sum(d_hidden * norm_two, axis=0)
    norm_two_pull = jax.vjp(layer_norm, resid)[1]
    d_resid = cotangent + norm_two_pull(d_hidden * gain_two)[0]
    d_attn = (d_resid * valid_f).astype(BF)
    grad_attention_out = jnp.dot(heads_out.T, d_attn, preferred_element_type=F32)
    early = jnp.concatenate(
        [
            grad_attention_out.reshape(devices, o_rows, width),
            pad_to(
                jnp.concatenate(
                    [
                        grad_router.reshape(devices, router_size),
                        grad_gain_two.reshape(devices, gain_rows),
                    ],
                    axis=1,
                ),
                small_rows * width,
            ).reshape(devices, small_rows, width),
        ],
        axis=1,
    )
    early = lax.psum_scatter(early, BOTH, scatter_dimension=0, tiled=False)
    d_heads = jnp.dot(d_attn, attention_out.T, preferred_element_type=F32).astype(BF)
    d_query, d_key, d_value = attend_backward(
        query, key_rows, value_rows, d_heads, segment, valid, log_sums, head_count
    )
    d_projected = jnp.stack([d_query, d_key, d_value], axis=0)
    grad_projections = jnp.einsum(
        "td,jte->jde", act, d_projected, preferred_element_type=F32
    ).reshape(devices, q_rows, width)
    d_act = jnp.einsum("jte,jde->td", d_projected, projection_stack, preferred_element_type=F32)
    grad_gain_one = jnp.sum(d_act * norm_one, axis=0)
    late = jnp.concatenate(
        [
            grad_projections,
            pad_to(grad_gain_one.reshape(devices, 1, gain_rows), width),
        ],
        axis=1,
    )
    late = lax.psum_scatter(late, BOTH, scatter_dimension=0, tiled=False)
    norm_one_pull = jax.vjp(layer_norm, tokens_f)[1]
    tokens_grad = (d_resid + norm_one_pull(d_act * gain_one)[0]).astype(BF)
    early_tail = early[o_rows:].reshape(-1)
    return (
        output,
        tokens_grad,
        late[q_rows, :gain_rows],
        late[:q_rows],
        early[:o_rows],
        early_tail[router_size : router_size + gain_rows],
        early_tail[:router_size].reshape(gain_rows, expert_count),
        grad_train_in,
        grad_train_out,
    )


def solution(mesh):
    rows = P(("dp", "expert"), None)
    flat = P(("dp", "expert"))
    expert = P("expert", None, "dp")
    return jax.shard_map(
        local,
        mesh=mesh,
        in_specs=(
            rows, flat, flat, rows, rows, flat, rows, rows, flat, rows,
            expert, expert, expert, expert,
        ),
        out_specs=(rows, rows, flat, rows, rows, flat, rows, expert, expert),
        check_vma=False,
    )
```

time: 1340 us -> 1030 us (0.77)
  matrix products: 296 us -> 134 us
  Pallas kernels: 0 us -> 153 us
  blocking collectives: 326 us -> 191 us
  local copies, waits for them, and re-layouts: 144 us -> 41.9 us
  other arithmetic: 180 us -> 103 us
    dot_general x18 -> x8, matrix products: 192 us -> 22.7 us  [the longest x1 5.96 us: local(): jnp.einsum('td,jte->jde', act, d_projected, preferred_element_type=F32)]
    pallas_call x0 -> x6, Pallas kernels: none -> 153 us  [the longest x2 107 us: run_experts(): pl.pallas_call(functools.partial(expert_kernel, train=train, chunk=chunk,...]
    all_gather x1 -> x0, blocking collectives: 140 us -> none  [local(): lax.all_gather(router.astype(jnp.bfloat16), ('dp', 'expert'), axis=0, til...]
    all_to_all x3 -> x5, waiting for transfers between devices: 201 us -> 77.3 us  [swap(): lax.all_to_all(rows, 'expert', split_axis=0, concat_axis=0, tiled=True)]
    reduce_scatter x4, waiting for transfers between devices: 103 us -> 209 us  [the longest x1 76.6 us: local(): lax.psum_scatter(grad_in, 'dp', scatter_dimension=0, tiled=False)]
    all_to_all x1 -> x3, blocking collectives: 105 us -> 191 us  [swap(): lax.all_to_all(rows, 'expert', split_axis=0, concat_axis=0, tiled=True)]
    unnamed x2 -> x0, blocking collectives: 81.1 us -> none
    gather x4 -> x0, local copies, waits for them, and re-layouts: 40.3 us -> none  [the longest x2 20.8 us: local(): d_taken = jnp.take(d_returned, dest, axis=0, mode='fill', fill_value=0)]
  transfers between devices with their start and end apart: 14 -> 14, of which waited for: 4 -> 8; matrix products, arithmetic and copies ran while one was open for 37% -> 14% of each run, Pallas kernels for 0% -> 14%
where the time goes in v1:
time: 1030 us; the launch traced here: 1020 us
  waiting for transfers between devices  359 us (35%)
  blocking collectives  191 us (19%)
  Pallas kernels  153 us (15%)
  matrix products  134 us (13%)
  other arithmetic  103 us (10%)
  local copies, waits for them, and re-layouts  41.9 us (4%)
  starting transfers between devices  27 us (3%)
  between operations  15.2 us (1%)
    all_to_all x3, blocking collectives, swap(): lax.all_to_all(rows, 'expert', split_axis=0, concat_axis=0, tiled=True)  191 us
    pallas_call x2, Pallas kernels, run_experts(): pl.pallas_call(functools.partial(expert_kernel, train=train, chunk=chunk,...  107 us
    all_to_all x5, waiting for transfers between devices, swap(): lax.all_to_all(rows, 'expert', split_axis=0, concat_axis=0, tiled=True)  77.3 us
    reduce_scatter x1, waiting for transfers between devices, local(): lax.psum_scatter(grad_in, 'dp', scatter_dimension=0, tiled=False)  76.6 us
    reduce_scatter x1, waiting for transfers between devices, local(): lax.psum_scatter(grad_out, 'dp', scatter_dimension=0, tiled=False)  76.4 us
    all_gather x1, waiting for transfers between devices, local(): dense = lax.all_gather(payload, BOTH, axis=0, tiled=False)  61.3 us
    reduce_scatter x1, waiting for transfers between devices, local(): late = lax.psum_scatter(late, BOTH, scatter_dimension=0, tiled=False)  56 us
    convert_element_type x2, other arithmetic, attend_backward(): d_scores = (attention * (d_attention - jnp.sum(d_attention * attention, a...  29.5 us
  transfers between devices with their start and end apart: 14, of which 8 were waited for; matrix products, arithmetic and copies ran while one was open for 14% of the time, Pallas kernels for 14%

profile of v1, /device:TPU:0, one launch (start us, length us, event | category | flops | bytes accessed | tf_op | source)
XLA Modules:
  0.0 1024.6 jit_solution(4827441133331548412)
XLA Ops:
  12.1 4.0 convert_element_type.180
  16.1 4.0 convert_element_type.181
  20.2 4.0 convert_element_type.182
  26.3 12.6 %first_dispatch.1 = (s32[32,1024]{1,0:T(8,128)}, s32[1024,128]{1,0:T(8,128)}, bf16[8,192,768]{2,1,0:T(8,128)(2,1)}, bf16[8,192,768]{2,1,0:T(8,128)(2,1)}) custom-call(s32[1024,2]{1,0:T(8,128)} %copy.82.routes_ref, s32[2,1024]{1,0:T(2,128)} %bitcast.176, s32[1024,1]{1,0:T(8,128)} %copy.83.valid_ref, s32[1,1024]{1,0:T(1,128)} %bitcast.174, ...), custom_call_target="tpu_custom_call" | custom-call | flops 4831838208 | bytes 8000000 | tf_op jit(solution)/shard_map/first_dispatch/pallas_call | solution.py:213
  38.9 7.4 all-to-all-start.1
  46.4 4.1 convert_element_type.183
  52.5 61.3 %all-gather.10.cloned.1.call-done = bf16[32,98,768]{2,1,0:T(8,128)(2,1)} async-done(((bf16[1,98,768]{2,1,0:T(8,128)(2,1)}), bf16[32,98,768]{2,1,0:T(8,128)(2,1)}) %all-gather.10.cloned.1.call-update) | async-done | bytes 4816912 | tf_op jit(solution)/shard_map/all_gather | solution.py:549
  115.0 2.2 slice.217
  117.3 5.0 convert_bitcast_fusion
  124.9 10.7 %fusion.8 = (f32[12,512]{1,0:T(8,128)S(1)}, f32[12,512,1024]{2,1,0:T(8,128)}) fusion(pred[512,1024]{1,0:T(8,128)(4,1)S(1)} %fusion.27, bf16[512,12,64]{0,2,1:T(8,128)(2,1)S(1)} %bitcast.137, bf16[1024,12,64]{0,2,1:T(8,128)(2,1)S(1)} %bitcast.133), kind=kOutput, calls=%fused_computation.19 | convolution fusion | flops 824174592 | bytes 28073984 | tf_op jit(solution)/shard_map/qhd,khd->hqk/dot_general | solution.py:46
  135.6 11.9 %fusion = f32[12,512]{1,0:T(8,128)S(1)} fusion(f32[12,512]{1,0:T(8,128)S(1)} %get-tuple-element.125, f32[12,512,1024]{2,1,0:T(8,128)} %get-tuple-element.126, pred[512,1024]{1,0:T(8,128)(4,1)S(1)} %fusion.27), kind=kLoop, calls=%fused_computation.6 | loop fusion | flops 25159680 | bytes 25739264 | tf_op jit(solution)/shard_map/reduce_sum | solution.py:54
  147.5 2.1 fusion.17
  149.7 2.6 fusion.6
  152.3 2.1 copy-done
  154.4 13.3 %fusion.35 = bf16[12,64,512]{2,1,0:T(8,128)(2,1)} fusion(bf16[1024,12,64]{0,2,1:T(8,128)(2,1)S(1)} %bitcast.145, f32[12,512]{1,0:T(8,128)S(1)} %fusion, f32[12,512]{1,0:T(8,128)S(1)} %get-tuple-element.125, f32[12,512,1024]{2,1,0:T(8,128)} %get-tuple-element.126, pred[512,1024]{1,0:T(8,128)(4,1)S(1)} %fusion.27), kind=kOutput, calls=%fused_computation.70 | convolution fusion | flops 837156864 | bytes 28098560 | tf_op jit(solution)/shard_map/hqk,khd->qhd/dot_general | solution.py:56
  167.8 4.4 all-to-all-start.4
  172.2 7.6 fusion.34
  182.1 4.2 fusion.72
  193.0 2.2 fusion.49
  197.5 1.9 copy.89.gate_ref
  199.4 10.5 %second_dispatch.1 = (bf16[8,208,768]{2,1,0:T(8,128)(2,1)}, bf16[8,208,768]{2,1,0:T(8,128)(2,1)}) custom-call(s32[32,1024]{1,0:T(8,128)} %get-tuple-element.88.slot_ref, f32[32,1024]{1,0:T(8,128)} %copy.89.gate_ref, bf16[1024,768]{1,0:T(8,128)(2,1)} %copy-done.7), custom_call_target="tpu_custom_call" | custom-call | flops 4831838208 | bytes 8000000 | tf_op jit(solution)/shard_map/second_dispatch/pallas_call | solution.py:275
  209.9 16.8 %all-to-all-done.4.refs_1_ = bf16[8,192,768]{2,1,0:T(8,128)(2,1)} async-done(((bf16[8,192,768]{2,1,0:T(8,128)(2,1)}), bf16[8,192,768]{2,1,0:T(8,128)(2,1)}, u32[]{:S(2)}, u32[]{:S(2)}) %all-to-all-start.4) | async-done | bytes 2359328 | tf_op jit(solution)/shard_map/all_to_all | solution.py:515
  226.7 62.4 %all_to_all.40.refs_0_ = bf16[8,208,768]{2,1,0:T(8,128)(2,1)} all-to-all(bf16[8,208,768]{2,1,0:T(8,128)(2,1)} %get-tuple-element.89), channel_id=1, replica_groups=mesh['dp'=4,'expert'=8] {'expert'}, dimensions={0} | all-to-all | bytes 5111808 | tf_op jit(solution)/shard_map/all_to_all | solution.py:515
  289.1 4.6 all-to-all-start.3
  293.7 64.0 %experts_train.1 = (bf16[8,192,768]{2,1,0:T(8,128)(2,1)}, bf16[8,208,768]{2,1,0:T(8,128)(2,1)}, bf16[4,2,768,768]{3,2,1,0:T(8,128)(2,1)}, bf16[4,2,768,768]{3,2,1,0:T(8,128)(2,1)}) custom-call(bf16[8,208,768]{2,1,0:T(8,128)(2,1)} %all_to_all.40.refs_0_, bf16[8,192,768]{2,1,0:T(8,128)(2,1)} %all-to-all-done.1.refs_1_, bf16[4,2,768,768]{3,2,1,0:T(8,128)(2,1)} %bitcast.178, ...), custom_call_target="tpu_custom_call" | custom-call | flops 43486543872 | bytes 30000000 | tf_op jit(solution)/shard_map/experts_train/pallas_call | solution.py:408
  357.7 5.9 all-to-all-start.6
  363.7 9.8 all-gather.18.cloned.1.call-done
  373.6 43.1 %experts_frozen.1 = (bf16[8,192,768]{2,1,0:T(8,128)(2,1)}, bf16[8,208,768]{2,1,0:T(8,128)(2,1)}) custom-call(bf16[8,208,768]{2,1,0:T(8,128)(2,1)} %all-to-all-done.3.refs_0_, bf16[8,192,768]{2,1,0:T(8,128)(2,1)} %all-to-all-done.4.refs_1_, bf16[4,2,768,768]{3,2,1,0:T(8,128)(2,1)} %bitcast.177, bf16[4,2,768,768]{3,2,1,0:T(8,128)(2,1)} %bitcast.180), custom_call_target="tpu_custom_call" | custom-call | flops 28991029248 | bytes 30000000 | tf_op jit(solution)/shard_map/experts_frozen/pallas_call | solution.py:408
  416.7 3.8 all-to-all-done.6
  420.4 4.4 all-to-all-start.7
  425.7 56.7 %all-to-all-done.7 = bf16[8,208,768]{2,1,0:T(8,128)(2,1)} async-done(((bf16[8,208,768]{2,1,0:T(8,128)(2,1)}), bf16[8,208,768]{2,1,0:T(8,128)(2,1)}, u32[]{:S(2)}, u32[]{:S(2)}) %all-to-all-start.7) | async-done | bytes 2555936 | tf_op jit(solution)/shard_map/all_to_all | solution.py:515
  482.4 13.3 %combine_back.1 = (f32[1024,768]{1,0:T(8,128)}, f32[1024,128]{1,0:T(8,128)}) custom-call(s32[1024,128]{1,0:T(8,128)} %get-tuple-element.87.dest_ref, bf16[1664,768]{1,0:T(8,128)(2,1)} %bitcast.28.a_ref, bf16[1664,768]{1,0:T(8,128)(2,1)} %bitcast.29.b_ref), custom_call_target="tpu_custom_call" | custom-call | flops 5234491392 | bytes 12000000 | tf_op jit(solution)/shard_map/combine_back/pallas_call | solution.py:468
  495.8 2.2 multiply_reduce_fusion.6
  498.0 2.2 multiply_reduce_fusion.5
  503.3 1.7 copy-done.3
  508.8 4.1 fusion.31
  512.9 7.2 multiply_reduce_fusion.1
  521.4 2.8 fusion.38
  524.3 20.2 %multiply_reduce_fusion = (f32[12,512]{1,0:T(8,128)S(1)}, f32[12,512,1024]{2,1,0:T(8,128)}) fusion(f32[12,512]{1,0:T(8,128)S(1)} %log_add_fusion, f32[12,512,1024]{2,1,0:T(8,128)} %get-tuple-element.126, pred[512,1024]{1,0:T(8,128)(4,1)S(1)} %copy-done.11, bf16[512,12,64]{0,2,1:T(8,128)(2,1)S(1)} %bitcast.153, bf16[1024,12,64]{0,2,1:T(8,128)(2,1)} %bitcast.144), kind=kOutput, calls=%fused_computation.1 | convolution fusion | flops 836757504 | bytes 53264384 | tf_op jit(solution)/shard_map/qhd,khd->hqk/dot_general | solution.py:85
  544.5 13.4 %fusion.24 = bf16[1024,12,64]{0,2,1:T(8,128)(2,1)} fusion(f32[512,12,64]{0,2,1:T(8,128)} %fusion.31, bf16[512,12,64]{0,2,1:T(8,128)(2,1)S(1)} %bitcast.154, f32[12,512]{1,0:T(8,128)S(1)} %log_add_fusion, f32[12,512,1024]{2,1,0:T(8,128)} %get-tuple-element.126, pred[512,1024]{1,0:T(8,128)(4,1)S(1)} %copy-done.11), kind=kOutput, calls=%fused_computation.46 | convolution fusion | flops 832045056 | bytes 29646848 | tf_op jit(solution)/shard_map/hqk,qhd->khd/dot_general | solution.py:102
  557.9 13.5 %multiply_convert_fusion.1 = bf16[12,512,512]{1,2,0:T(8,128)(2,1)} fusion(f32[12,512,512]{1,2,0:T(8,128)} %get-tuple-element.135, f32[12,512]{1,0:T(8,128)S(1)} %get-tuple-element.134, f32[12,512]{1,0:T(8,128)S(1)} %log_add_fusion.1, f32[12,512,512]{1,2,0:T(8,128)} %copy-done, pred[512,512]{0,1:T(8,128)(4,1)S(1)} %fusion.37), kind=kLoop, calls=%fused_computation.10 | loop fusion | flops 18874368 | bytes 31768576 | tf_op jit(solution)/shard_map/convert_element_type | solution.py:90
  571.4 5.9 multiply_bitcast_fusion
  577.4 16.0 %multiply_convert_fusion = bf16[12,512,1024]{2,1,0:T(8,128)(2,1)} fusion(f32[12,512,1024]{2,1,0:T(8,128)} %get-tuple-element.137, f32[12,512]{1,0:T(8,128)S(1)} %get-tuple-element.136, f32[12,512]{1,0:T(8,128)S(1)} %log_add_fusion, f32[12,512,1024]{2,1,0:T(8,128)S(1)} %bitcast.130, pred[512,1024]{1,0:T(8,128)(4,1)S(1)} %copy-done.11), kind=kLoop, calls=%fused_computation | loop fusion | flops 37748736 | bytes 63488000 | tf_op jit(solution)/shard_map/convert_element_type | solution.py:90
  593.4 10.1 multiply_convert_fusion.4
  603.5 5.1 fusion.25
  609.0 3.8 pad_maximum_fusion.1
  612.9 4.8 multiply_convert_fusion.5
  617.7 2.8 copy.98
  622.2 2.4 copy.94
  624.6 2.3 copy.93
  627.0 7.1 fusion.23
  635.8 1.7 fusion.21
  637.6 6.0 fusion.39
  643.5 4.1 select_maximum_fusion
  650.2 71.6 %all_to_all.41 = bf16[8,192,768]{2,1,0:T(8,128)(2,1)} all-to-all(bf16[8,192,768]{2,1,0:T(8,128)(2,1)S(1)} %copy-done.27), channel_id=1, replica_groups=mesh['dp'=4,'expert'=8] {'expert'}, dimensions={0} | all-to-all | bytes 4718592 | tf_op jit(solution)/shard_map/all_to_all | solution.py:515
  721.8 57.1 %all_to_all.42 = bf16[8,192,768]{2,1,0:T(8,128)(2,1)} all-to-all(bf16[8,192,768]{2,1,0:T(8,128)(2,1)S(1)} %copy-done.28), channel_id=1, replica_groups=mesh['dp'=4,'expert'=8] {'expert'}, dimensions={0} | all-to-all | bytes 4718592 | tf_op jit(solution)/shard_map/all_to_all | solution.py:515
  778.9 9.9 combine_out.1
  788.8 4.6 add_convert_fusion
  797.6 56.0 %reduce-scatter.5.cloned.1.call-done = f32[1,73,768]{2,1,0:T(8,128)} async-done(((f32[32,73,768]{2,1,0:T(8,128)}), f32[1,73,768]{2,1,0:T(8,128)}) %reduce-scatter.5.cloned.1.call-update) | async-done | bytes 224272 | tf_op jit(solution)/shard_map/reduce_scatter | solution.py:658
  854.7 1.6 slice_bitcast_fusion
  856.4 76.6 %reduce-scatter.9.cloned.1.call-done = bf16[1,2,768,768]{3,2,1,0:T(8,128)(2,1)} async-done(((bf16[4,2,768,768]{3,2,1,0:T(8,128)(2,1)}), bf16[1,2,768,768]{3,2,1,0:T(8,128)(2,1)}) %reduce-scatter.9.cloned.1.call-update) | async-done | bytes 2359312 | tf_op jit(solution)/shard_map/reduce_scatter | solution.py:606
  933.0 4.2 bitcast_convert_fusion.1
  937.2 76.4 %reduce-scatter.11.cloned.1.call-done = bf16[1,2,768,768]{3,2,1,0:T(8,128)(2,1)} async-done(((bf16[4,2,768,768]{3,2,1,0:T(8,128)(2,1)}), bf16[1,2,768,768]{3,2,1,0:T(8,128)(2,1)}) %reduce-scatter.11.cloned.1.call-update) | async-done | bytes 2359312 | tf_op jit(solution)/shard_map/reduce_scatter | solution.py:607
  1013.6 4.2 bitcast_convert_fusion
  (242 shorter events, 44.7 us)
Async XLA Ops:
  7.2 106.5 %all-gather.10.cloned.1.call-start = ((), (), s32[]{:S(2)}) async-start(), calls=%async_computation.12 | async-start | bytes 5271552 | tf_op jit(solution)/shard_map/all_gather | solution.py:549
  12.0 281.7 %all-gather.12.cloned.1.call-start = ((), (), s32[]{:S(2)}) async-start(), calls=%async_computation.17 | async-start | bytes 11796480 | tf_op jit(solution)/shard_map/all_gather | solution.py:570
  16.1 277.7 %all-gather.14.cloned.1.call-start = ((), (), s32[]{:S(2)}) async-start(), calls=%async_computation.18 | async-start | bytes 11796480 | tf_op jit(solution)/shard_map/all_gather | solution.py:570
  20.1 5.1 copy-start.48
  20.2 343.5 %all-gather.16.cloned.1.call-start = ((), (), s32[]{:S(2)}) async-start(), calls=%async_computation.19 | async-start | bytes 11796480 | tf_op jit(solution)/shard_map/all_gather | solution.py:570
  38.9 128.9 %all-to-all-start.1 = ((bf16[8,192,768]{2,1,0:T(8,128)(2,1)}), bf16[8,192,768]{2,1,0:T(8,128)(2,1)}, u32[]{:S(2)}, u32[]{:S(2)}) async-start(bf16[8,192,768]{2,1,0:T(8,128)(2,1)} %get-tuple-element.90), calls=%async_computation.1 | async-start | bytes 4718592 | tf_op jit(solution)/shard_map/all_to_all | solution.py:515
  46.3 327.2 %all-gather.18.cloned.1.call-start = ((), (), s32[]{:S(2)}) async-start(), calls=%async_computation.20 | async-start | bytes 11796480 | tf_op jit(solution)/shard_map/all_gather | solution.py:570
  50.6 131.5 %copy-start.53 = (f32[1024]{0:T(1024)}, f32[1024]{0:T(1024)S(1)}, u32[]{:S(2)}) copy-start(f32[1024]{0:T(1024)S(1)} %convert_element_type.176) | copy-start | bytes 12292
  50.9 66.3 %copy-start.42 = (f32[1024]{0:T(1024)}, f32[1024]{0:T(1024)S(1)}, u32[]{:S(2)}) copy-start(f32[1024]{0:T(1024)S(1)} %broadcast_multiply_fusion.1) | copy-start | bytes 12292
  51.5 65.7 %copy-start.57 = (f32[1024]{0:T(1024)}, f32[1024]{0:T(1024)S(1)}, u32[]{:S(2)}) copy-start(f32[1024]{0:T(1024)S(1)} %fusion.22) | copy-start | bytes 12292
  51.5 65.7 %copy-start.55 = (f32[1024]{0:T(1024)}, f32[1024]{0:T(1024)S(1)}, u32[]{:S(2)}) copy-start(f32[1024]{0:T(1024)S(1)} %fusion.50) | copy-start | bytes 12292
  52.4 102.0 %copy-start.10 = (pred[512,1024]{1,0:T(8,128)(4,1)}, pred[512,1024]{1,0:T(8,128)(4,1)S(1)}, u32[]{:S(2)}) copy-start(pred[512,1024]{1,0:T(8,128)(4,1)S(1)} %fusion.27) | copy-start | bytes 1572868
  117.2 5.1 copy-start.23
  124.0 11.6 %copy-start.17 = (bf16[1,512,768]{1,2,0:T(8,128)(2,1)}, bf16[1,512,768]{1,2,0:T(8,128)(2,1)S(1)}, u32[]{:S(2)}) copy-start(bf16[1,512,768]{1,2,0:T(8,128)(2,1)S(1)} %get-tuple-element.112) | copy-start | bytes 2359300
  124.0 23.5 %copy-start.15 = (bf16[1,512,768]{1,2,0:T(8,128)(2,1)}, bf16[1,512,768]{1,2,0:T(8,128)(2,1)S(1)}, u32[]{:S(2)}) copy-start(bf16[1,512,768]{1,2,0:T(8,128)(2,1)S(1)} %get-tuple-element.111) | copy-start | bytes 2359300
  124.1 23.5 %copy-start.19 = (bf16[1,512,768]{1,2,0:T(8,128)(2,1)}, bf16[1,512,768]{1,2,0:T(8,128)(2,1)S(1)}, u32[]{:S(2)}) copy-start(bf16[1,512,768]{1,2,0:T(8,128)(2,1)S(1)} %get-tuple-element.113) | copy-start | bytes 2359300
  124.1 48.1 %copy-start.24 = (bf16[1,512,768]{1,2,0:T(8,128)(2,1)}, bf16[1,512,768]{1,2,0:T(8,128)(2,1)S(1)}, u32[]{:S(2)}) copy-start(bf16[1,512,768]{1,2,0:T(8,128)(2,1)S(1)} %get-tuple-element.114) | copy-start | bytes 2359300
  135.6 18.8 %copy-start.35 = (f32[12,512]{1,0:T(8,128)}, f32[12,512]{1,0:T(8,128)S(1)}, u32[]{:S(2)}) copy-start(f32[12,512]{1,0:T(8,128)S(1)} %get-tuple-element.125) | copy-start | bytes 73732
  147.5 6.9 copy-start.39
  149.6 4.8 copy-start
  149.7 22.5 %copy-start.37 = (f32[12,512]{1,0:T(8,128)}, f32[12,512]{1,0:T(8,128)S(1)}, u32[]{:S(2)}) copy-start(f32[12,512]{1,0:T(8,128)S(1)} %get-tuple-element.127) | copy-start | bytes 73732
  149.7 4.7 copy-start.21
  154.4 17.8 %copy-start.41 = (f32[12,512]{1,0:T(8,128)}, f32[12,512]{1,0:T(8,128)S(1)}, u32[]{:S(2)}) copy-start(f32[12,512]{1,0:T(8,128)S(1)} %fusion.6) | copy-start | bytes 73732
  167.8 58.9 %all-to-all-start.4 = ((bf16[8,192,768]{2,1,0:T(8,128)(2,1)}), bf16[8,192,768]{2,1,0:T(8,128)(2,1)}, u32[]{:S(2)}, u32[]{:S(2)}) async-start(bf16[8,192,768]{2,1,0:T(8,128)(2,1)} %get-tuple-element.93), calls=%async_computation.4 | async-start | bytes 4718592 | tf_op jit(solution)/shard_map/all_to_all | solution.py:515
  179.9 7.0 copy-start.44
  186.4 315.4 %copy-start.2 = (f32[1024,768]{1,0:T(8,128)}, f32[1024,768]{1,0:T(8,128)S(1)}, u32[]{:S(2)}) copy-start(f32[1024,768]{1,0:T(8,128)S(1)} %get-tuple-element.130.resid_ref) | copy-start | bytes 9437188
  289.1 68.6 %all-to-all-start.3 = ((bf16[8,208,768]{2,1,0:T(8,128)(2,1)}), bf16[8,208,768]{2,1,0:T(8,128)(2,1)}, u32[]{:S(2)}, u32[]{:S(2)}) async-start(bf16[8,208,768]{2,1,0:T(8,128)(2,1)} %get-tuple-element.92), calls=%async_computation.3 | async-start | bytes 5111808 | tf_op jit(solution)/shard_map/all_to_all | solution.py:515
  357.7 62.7 %all-to-all-start.6 = ((bf16[8,208,768]{2,1,0:T(8,128)(2,1)}), bf16[8,208,768]{2,1,0:T(8,128)(2,1)}, u32[]{:S(2)}, u32[]{:S(2)}) async-start(bf16[8,208,768]{2,1,0:T(8,128)(2,1)} %get-tuple-element.95), calls=%async_computation.6 | async-start | bytes 5111808 | tf_op jit(solution)/shard_map/all_to_all | solution.py:515
  416.7 8.2 copy-start.38
  416.7 9.0 copy-start.36
  416.7 9.0 copy-start.40
  420.4 62.0 %all-to-all-start.7 = ((bf16[8,208,768]{2,1,0:T(8,128)(2,1)}), bf16[8,208,768]{2,1,0:T(8,128)(2,1)}, u32[]{:S(2)}, u32[]{:S(2)}) async-start(bf16[8,208,768]{2,1,0:T(8,128)(2,1)} %get-tuple-element.96), calls=%async_computation.7 | async-start | bytes 5111808 | tf_op jit(solution)/shard_map/all_to_all | solution.py:515
  424.8 368.5 %reduce-scatter.7.cloned.1.call-start = ((), (), s32[]{:S(2)}) async-start(), calls=%async_computation.14 | async-start | bytes 3244032 | tf_op jit(solution)/shard_map/reduce_scatter | solution.py:640
  495.8 4.4 copy-start.13
  495.8 4.6 copy-start.26
  495.8 4.6 copy-start.30
  495.8 4.6 copy-start.45
  495.8 4.6 copy-start.47
  500.4 4.6 copy-start.22
  501.8 6.4 slice-start.6
  501.8 6.4 slice-start.7
  512.9 7.2 copy-start.8
  512.9 8.5 copy-start.64
  512.9 8.5 copy-start.65
  544.5 32.9 %slice-start = ((s8[25165824]{0:T(1024)(128)(4,1)}), s8[4194304]{0:T(1024)(128)(4,1)S(1)}, s32[]{:S(2)}) async-start(s8[25165824]{0:T(1024)(128)(4,1)} %bitcast.129), calls=%async_computation.21 | async-start | bytes 8388608
  544.5 32.9 %slice-start.1 = ((s8[25165824]{0:T(1024)(128)(4,1)}), s8[4194304]{0:T(1024)(128)(4,1)S(1)}, s32[]{:S(2)}) async-start(s8[25165824]{0:T(1024)(128)(4,1)} %bitcast.129), calls=%async_computation.22 | async-start | bytes 8388608
  544.5 32.9 %slice-start.2 = ((s8[25165824]{0:T(1024)(128)(4,1)}), s8[4194304]{0:T(1024)(128)(4,1)S(1)}, s32[]{:S(2)}) async-start(s8[25165824]{0:T(1024)(128)(4,1)} %bitcast.129), calls=%async_computation.23 | async-start | bytes 8388608
  557.9 13.5 %copy-start.20 = (bf16[1,512,768]{1,2,0:T(8,128)(2,1)S(1)}, bf16[1,512,768]{1,2,0:T(8,128)(2,1)}, u32[]{:S(2)}) copy-start(bf16[1,512,768]{1,2,0:T(8,128)(2,1)} %copy-done.19) | copy-start | bytes 2359300
  557.9 19.5 %slice-start.3 = ((s8[25165824]{0:T(1024)(128)(4,1)}), s8[4194304]{0:T(1024)(128)(4,1)S(1)}, s32[]{:S(2)}) async-start(s8[25165824]{0:T(1024)(128)(4,1)} %bitcast.129), calls=%async_computation.24 | async-start | bytes 8388608
  557.9 19.5 %slice-start.4 = ((s8[25165824]{0:T(1024)(128)(4,1)}), s8[4194304]{0:T(1024)(128)(4,1)S(1)}, s32[]{:S(2)}) async-start(s8[25165824]{0:T(1024)(128)(4,1)} %bitcast.129), calls=%async_computation.25 | async-start | bytes 8388608
  557.9 19.5 %slice-start.5 = ((s8[25165824]{0:T(1024)(128)(4,1)}), s8[4194304]{0:T(1024)(128)(4,1)S(1)}, s32[]{:S(2)}) async-start(s8[25165824]{0:T(1024)(128)(4,1)} %bitcast.129), calls=%async_computation.26 | async-start | bytes 8388608
  593.4 10.1 copy-start.1
  603.5 5.2 copy-start.32
  612.9 240.7 %reduce-scatter.5.cloned.1.call-start = ((), (), s32[]{:S(2)}) async-start(), calls=%async_computation.13 | async-start | bytes 8110080 | tf_op jit(solution)/shard_map/reduce_scatter | solution.py:658
  620.6 6.4 copy-start.6
  620.6 6.4 copy-start.43
  620.6 6.4 copy-start.52
  622.2 4.8 copy-start.31
  627.0 7.2 copy-start.58
  627.0 8.8 copy-start.56
  647.7 285.4 %reduce-scatter.9.cloned.1.call-start = ((), (), s32[]{:S(2)}) async-start(), calls=%async_computation.15 | async-start | bytes 11796480 | tf_op jit(solution)/shard_map/reduce_scatter | solution.py:606
  648.4 365.2 %reduce-scatter.11.cloned.1.call-start = ((), (), s32[]{:S(2)}) async-start(), calls=%async_computation.16 | async-start | bytes 11796480 | tf_op jit(solution)/shard_map/reduce_scatter | solution.py:607
  649.1 72.7 %copy-start.28 = (bf16[8,192,768]{2,1,0:T(8,128)(2,1)S(1)}, bf16[8,192,768]{2,1,0:T(8,128)(2,1)}, u32[]{:S(2)}) copy-start(bf16[8,192,768]{2,1,0:T(8,128)(2,1)} %get-tuple-element.94) | copy-start | bytes 7077892
  778.9 9.9 copy-start.4
  (25 other events, 61.7 us)
Sparse Core Ops, SparseCore 0:
  12.1 101.5 all-gather.9
  115.3 61.0 all-gather.11
  178.0 64.1 all-gather.13
  243.6 64.2 all-gather.15
  309.3 64.2 all-gather.17
  613.0 112.2 reduce-scatter.6
  731.0 122.5 reduce-scatter.4
  856.1 76.8 reduce-scatter.8
  935.6 77.9 reduce-scatter.10
